TPU v7x, 256 devices: a whole 4x4x8 slice. The times are simulated.
256 devices in a mesh: lat: 4 (over z_hi), lon: 64 (over x, y, z_lo, core).
Axes of the slice: x: 4, y: 4, z: 8 (z_hi: 4, z_lo: 2; z = z_hi * 2 + z_lo), core: 2. Of those that a mesh axis runs over, the one named last changes fastest.
Arguments:
- poleward_flow: float32 [10, 4, 256, 8192], P(None, None, 'lat', 'lon'), may hold values from -16 to 16
- potential_warmth: float32 [10, 4, 256, 8192], P(None, None, 'lat', 'lon'), may hold values from -16 to 16
- water_profile_flag: int32 [256, 8192], P('lat', 'lon'), may hold values from 0 to 1
- floor_count: int32 [256, 8192], P('lat', 'lon'), may hold values from 0 to 4, as said below
- catchment_label_for_site: int32 [256, 8192], P('lat', 'lon'), may hold values from 0 to 9
Outputs:
- eddy_temp: float32 [4, 256, 8192], P(None, 'lat', 'lon')
- transport: float32 [4, 10, 4, 256], P(None, None, None, ('lat', 'lon'))
Inputs may be any that keep to these rules, and one draw needn't show every extreme that they name: `floor_count`: land rows of zeros occur at some latitudes; elsewhere columns have 1 to 4 wet levels.
All inputs are finite; a program needn't handle non-finite values.
Results may differ from a plain program's by a relative error of at most 0.0003.
Values sent between devices are 32-bit elements; how exact they have to be, the bound alone decides.
A program may use at most 64 MiB of HBM per device.

v0:
```python
import math

import jax
import jax.numpy as jnp
from jax import lax
from jax.sharding import PartitionSpec as P

BASINS = 10


highest_accuracy = lax.Precision.HIGHEST


def shifted(block, axis, distance):
    devices = range(lax.axis_size(axis))
    route = [(i - distance, i) for i in devices if i - distance in devices]
    return lax.ppermute(block, axis, route)


def cut_along(x, dim, count):
    before, after = (x.shape[:dim], x.shape[dim + 1 :])
    return jnp.moveaxis(x.reshape(*before, count, -1, *after), dim, 0)


def sum_at_owner(x, axis, dim):
    count = lax.axis_size(axis)
    blocks = lax.all_to_all(cut_along(x, dim, count), axis, 0, 0, tiled=True)
    return jnp.sum(blocks, axis=0)


def side_by_side(arrays, axis, dim, along):
    ends, at = ([], 0)
    for a in arrays[:-1]:
        at += a.shape[along]
        ends.append(at)
    both = jnp.concatenate(arrays, axis=along)
    return tuple(jnp.split(sum_at_owner(both, axis, dim), ends, axis=along))


def laid_out(blocks, dim):
    blocks = jnp.moveaxis(blocks, 0, dim)
    shape = blocks.shape
    return blocks.reshape(*shape[:dim], shape[dim] * shape[dim + 1], *shape[dim + 2 :])


def copy_for_each(x, axis):
    count = lax.axis_size(axis)
    return lax.all_to_all(jnp.broadcast_to(x[None], (count, *x.shape)), axis, 0, 0, tiled=True)


def gathered_copies(x, axis, dim):
    return laid_out(copy_for_each(x, axis), dim)


def zonal_means(watered_total, along_latitude_totals):
    return along_latitude_totals / jnp.maximum(watered_total, 1.0)


def basin_cells(one_hot, per_basin):
    return jnp.einsum("bji,bkj->kji", one_hot, per_basin, precision=highest_accuracy)


def shards(
    poleward_flow, potential_warmth, water_profile_flag, floor_count, catchment_label_for_site
):
    snapshots, levels, lat_rows, lon_cols = poleward_flow.shape
    lon_devices = lax.axis_size("lon")
    scaling = 1.0 / math.sqrt(lon_cols * lon_devices)
    bottom_layer_limit = (water_profile_flag * floor_count).astype(jnp.float32)
    poleward_warmth, poleward_floor = shifted(
        (potential_warmth[:, :, 0, :], bottom_layer_limit[0]), "lat", -1
    )
    topmost_warmth = jnp.concatenate(
        [potential_warmth[:, :, 1:, :], poleward_warmth[:, :, None, :]], axis=2
    )
    warmth_entry = 0.5 * (potential_warmth + topmost_warmth)
    upper_depth = jnp.concatenate([bottom_layer_limit[1:], poleward_floor[None]], axis=0)
    level_values = jnp.arange(levels, dtype=jnp.float32)[:, None, None]
    wet_cells = (
        (level_values < bottom_layer_limit[None]) & (level_values < upper_depth[None])
    ).astype(jnp.float32)
    basin_ids = jnp.arange(BASINS, dtype=jnp.int32)
    one_hot = (catchment_label_for_site[None] == basin_ids[:, None, None]).astype(jnp.float32)
    scaling_factors = one_hot[:, None] * wet_cells[None]
    watered_total = jnp.sum(scaling_factors, axis=3)[None]
    along_latitude_flow = jnp.einsum(
        "yalq,falq->fyal", scaling_factors, poleward_flow, precision=highest_accuracy
    )
    along_latitude_warmth = jnp.einsum(
        "yalq,falq->fyal", scaling_factors, warmth_entry, precision=highest_accuracy
    )
    along_latitude_totals = jnp.concatenate([along_latitude_flow, along_latitude_warmth], axis=0)
    mean_velocity = jnp.mean(poleward_flow, axis=0)
    average_warmth = jnp.mean(warmth_entry, axis=0)
    cross_time = jnp.mean((poleward_flow - mean_velocity) * (warmth_entry - average_warmth), axis=0)
    product_sum = jnp.einsum(
        "bkji,kji->bkj", scaling_factors, mean_velocity * average_warmth, precision=highest_accuracy
    )
    cross_sum = jnp.einsum("bkji,kji->bkj", scaling_factors, cross_time, precision=highest_accuracy)
    stats = (watered_total, along_latitude_totals, jnp.stack([product_sum, cross_sum]))
    own_stats = side_by_side((stats[0], stats[1], stats[2]), "lon", 3, 0)
    own_means = zonal_means(own_stats[0], own_stats[1])
    every_bar_temp = gathered_copies(jnp.mean(own_means[snapshots:], axis=0), "lon", 2)
    own_count = own_stats[0][0]
    own_bar_v = jnp.mean(own_means[:snapshots], axis=0)
    own_bar_t = jnp.mean(own_means[snapshots:], axis=0)
    mean_flow = scaling * own_count * own_bar_v * own_bar_t
    swing_product = jnp.mean(
        (own_means[:snapshots] - own_bar_v) * (own_means[snapshots:] - own_bar_t), axis=0
    )
    zonal_swing = scaling * own_count * swing_product
    averaged_warmth_grid = basin_cells(one_hot, every_bar_temp)
    temp_star = average_warmth - averaged_warmth_grid
    eddy_temp = wet_cells * temp_star
    steady_share = scaling * (own_stats[2][0] - own_count * own_bar_v * own_bar_t)
    transient = scaling * own_stats[2][1] - zonal_swing
    transport = jnp.stack([mean_flow, steady_share, zonal_swing, transient])
    return (eddy_temp, transport)


def solution(mesh):
    return jax.shard_map(
        shards,
        mesh=mesh,
        in_specs=(
            P(None, None, "lat", "lon"),
            P(None, None, "lat", "lon"),
            P("lat", "lon"),
            P("lat", "lon"),
            P("lat", "lon"),
        ),
        out_specs=(P(None, "lat", "lon"), P(None, None, None, ("lat", "lon"))),
        check_vma=False,
    )
```

profile of v0, /device:TPU:193, one launch (start us, length us, event | category | flops | bytes accessed | tf_op | source)
XLA Modules:
  0.0 91.2 jit_solution(9036171122792521561)
XLA Ops:
  0.6 0.9 multiply_convert_fusion
  1.5 3.1 %collective-permute-start = (f32[128]{0:T(128)S(1)}, f32[128]{0:T(128)S(1)}, u32[]{:S(2)}, u32[]{:S(2)}) collective-permute-start(f32[128]{0:T(128)S(1)} %slice_bitcast_fusion), channel_id=1, source_target_pairs={{64,0},{128,64},{192,128},{65,1},{129,65},{193,129},{66,2},{130,66... | collective-permute-start | bytes 1544 | tf_op jit(solution)/shard_map/ppermute | solution.py:17
  4.6 1.5 %slice.40 = f32[10,4,1,128]{3,2,1,0:T(1,128)} slice(f32[10,4,64,128]{3,2,1,0:T(8,128)} %param.6), slice={[0:10], [0:4], [0:1], [0:128]} | slice | bytes 40960 | tf_op jit(solution)/shard_map/slice | solution.py:71
  6.2 2.5 %collective-permute-start.1 = (f32[10,4,128]{2,1,0:T(4,128)}, f32[10,4,128]{2,1,0:T(4,128)}, u32[]{:S(2)}, u32[]{:S(2)}) collective-permute-start(f32[10,4,128]{2,1,0:T(4,128)} %bitcast.2), channel_id=1, source_target_pairs={{64,0},{128,64},{192,128},{65,1},{129,65},{193,129},{66,2},{130,66... | collective-permute-start | bytes 61448 | tf_op jit(solution)/shard_map/ppermute | solution.py:17
  8.7 0.8 fusion.31
  9.5 2.5 %slice.39 = f32[10,4,63,128]{3,2,1,0:T(8,128)} slice(f32[10,4,64,128]{3,2,1,0:T(8,128)} %param.6), slice={[0:10], [0:4], [1:64], [0:128]} | slice | bytes 2580480 | tf_op jit(solution)/shard_map/slice | solution.py:74
  12.7 5.3 %fusion.10 = f32[10,10,4,64]{0,1,3,2:T(8,128)} fusion(f32[10,4,64,128]{3,2,1,0:T(8,128)S(1)} %copy-done, f32[4,64,128]{2,1,0:T(8,128)S(1)} %copy.62, f32[10,64,128]{2,0,1:T(8,128)S(1)} %fusion.31), kind=kOutput, calls=%fused_computation.11 | convolution fusion | flops 39649280 | bytes 1871872 | tf_op jit(solution)/shard_map/yalq,falq->fyal/dot_general | solution.py:86
  18.7 3.0 %copy.70 = f32[1,10,4,64]{0,1,3,2:T(8,128)} copy(f32[1,10,4,64]{1,3,2,0:T(8,128)S(1)} %bitcast.80) | data formatting | bytes 20480 | tf_op jit(solution)/shard_map/broadcast_in_dim | solution.py:85
  21.7 1.5 %fusion.42 = (f32[4,64,128]{2,1,0:T(8,128)S(1)}, f32[10,4,64,128]{3,2,1,0:T(8,128)S(1)}) fusion(f32[10,4,64,128]{3,2,1,0:T(8,128)S(1)} %copy-done.2, f32[10,4,1,128]{3,2,1,0:T(1,128)} %bitcast.3, f32[10,4,63,128]{3,2,1,0:T(8,128)} %slice.39), kind=kLoop, calls=%fused_computation.67 | loop fusion | flops 1277952 | bytes 4063232 | tf_op jit(solution)/shard_map/reduce_sum | solution.py:94
  23.5 5.4 %fusion.15 = f32[10,10,4,64]{0,1,3,2:T(8,128)} fusion(f32[10,4,64,128]{3,2,1,0:T(8,128)S(1)} %get-tuple-element.19, f32[4,64,128]{2,1,0:T(8,128)S(1)} %copy.62, f32[10,64,128]{2,0,1:T(8,128)S(1)} %fusion.31), kind=kOutput, calls=%fused_computation.12 | convolution fusion | flops 39649280 | bytes 1871872 | tf_op jit(solution)/shard_map/yalq,falq->fyal/dot_general | solution.py:89
  29.3 3.6 %fusion = f32[4,64,1,10]{3,2,1,0:T(1,128)S(1)} fusion(f32[4,64,128]{2,1,0:T(8,128)S(1)} %copy.62, f32[10,64,128]{2,0,1:T(8,128)S(1)} %fusion.31, f32[4,64,128,1]{2,0,1,3:T(4,128)S(1)} %bitcast.81), kind=kOutput, calls=%fused_computation | convolution fusion | flops 4259840 | bytes 600064 | tf_op jit(solution)/shard_map/bkji,kji->bkj/dot_general | solution.py:99
  33.0 2.2 %copy.72 = f32[1,10,4,64]{0,1,3,2:T(8,128)} copy(f32[1,10,4,64]{3,2,1,0:T(4,128)S(1)} %bitcast.82) | data formatting | bytes 20480 | tf_op jit(solution)/shard_map/stack | solution.py:100
  35.2 3.4 %fusion.2 = f32[4,64,1,10]{3,2,1,0:T(1,128)S(1)} fusion(f32[4,64,128]{2,1,0:T(8,128)S(1)} %copy.62, f32[10,64,128]{2,0,1:T(8,128)S(1)} %fusion.31, f32[4,64,128,1]{2,0,1,3:T(4,128)S(1)} %get-tuple-element.21), kind=kOutput, calls=%fused_computation.2 | convolution fusion | flops 4259840 | bytes 600064 | tf_op jit(solution)/shard_map/bkji,kji->bkj/dot_general | solution.py:96
  38.7 2.2 %copy.71 = f32[1,10,4,64]{0,1,3,2:T(8,128)} copy(f32[1,10,4,64]{3,2,1,0:T(4,128)S(1)} %bitcast.83) | data formatting | bytes 20480 | tf_op jit(solution)/shard_map/stack | solution.py:100
  40.8 7.7 %concatenate.11 = f32[23,10,4,64]{0,1,3,2:T(8,128)} concatenate(f32[1,10,4,64]{0,1,3,2:T(8,128)} %copy.70, f32[10,10,4,64]{0,1,3,2:T(8,128)S(1)} %copy-done.1, f32[10,10,4,64]{0,1,3,2:T(8,128)} %fusion.15, f32[1,10,4,64]{0,1,3,2:T(8,128)} %copy.71, f32[1,10,4,64]{0,1,3,2:T(8,128)} %copy.72), dimensions={0} | concatenate | bytes 471040 | tf_op jit(solution)/shard_map/concatenate | solution.py:36
  48.5 2.4 %copy.123 = f32[64,23,10,4,1]{1,3,4,2,0:T(4,128)S(1)} copy(f32[64,23,10,4,1]{1,2,0,3,4:T(8,128)} %bitcast.78) | data formatting | bytes 471040 | tf_op jit(solution)/shard_map/transpose | solution.py:22
  51.0 2.1 %reshape.209 = f32[64,1,920]{2,1,0:T(1,128)S(1)} reshape(f32[64,10,1,4,23]{4,3,2,1,0:T(4,128)S(1)} %bitcast.79) | data formatting | bytes 471040
  53.1 19.2 %all_to_all.10 = f32[64,1,920]{2,1,0:T(1,128)S(1)} all-to-all(f32[64,1,920]{2,1,0:T(1,128)S(1)} %reshape.209), channel_id=1, replica_groups=mesh['lat'=4,'lon'=64] {'lon'}, dimensions={0} | all-to-all | bytes 471040 | tf_op jit(solution)/shard_map/all_to_all | solution.py:27
  72.8 1.3 %reduce.16 = f32[64,920]{1,0:T(8,128)S(1)} reduce(f32[64,1,920]{2,1,0:T(1,128)S(1)} %all_to_all.10, f32[]{:T(128)} %broadcast.188), dimensions={1}, to_apply=%all_to_all.6.reduce_sub_computation | reduce | bytes 471044 | tf_op jit(solution)/shard_map/all_to_all | solution.py:27
  74.1 1.0 %reshape.210 = f32[64,10,1,4,23]{4,3,2,1,0:T(4,128)S(1)} reshape(f32[64,920]{1,0:T(8,128)S(1)} %reduce.16) | data formatting | bytes 471040
  76.3 0.7 broadcast_in_dim.11
  77.0 4.5 %all-to-all-start.1 = ((f32[64,10,4,1]{1,2,3,0:T(4,128)}), f32[64,10,4,1]{1,2,3,0:T(4,128)S(1)}, u32[]{:S(2)}, u32[]{:S(2)}) async-start(f32[64,10,4,1]{1,2,3,0:T(4,128)} %broadcast_in_dim.11), calls=%async_computation.1 | async-start | bytes 262144 | tf_op jit(solution)/shard_map/all_to_all | solution.py:48
  82.1 8.0 %all-to-all-done.1 = f32[64,10,4,1]{1,2,3,0:T(4,128)S(1)} async-done(((f32[64,10,4,1]{1,2,3,0:T(4,128)}), f32[64,10,4,1]{1,2,3,0:T(4,128)S(1)}, u32[]{:S(2)}, u32[]{:S(2)}) %all-to-all-start.1) | async-done | bytes 10272 | tf_op jit(solution)/shard_map/all_to_all | solution.py:48
  90.6 0.7 copy.76
  (48 shorter events, 4.9 us)
Async XLA Ops:
  0.6 11.4 %copy-start = (f32[10,4,64,128]{3,2,1,0:T(8,128)S(1)}, f32[10,4,64,128]{3,2,1,0:T(8,128)}, u32[]{:S(2)}) copy-start(f32[10,4,64,128]{3,2,1,0:T(8,128)} %param.5) | copy-start | bytes 3932164
  1.5 10.6 %copy-start.3 = (f32[64,128]{1,0:T(8,128)}, f32[64,128]{1,0:T(8,128)S(1)}, u32[]{:S(2)}) copy-start(f32[64,128]{1,0:T(8,128)S(1)} %multiply_convert_fusion) | copy-start | bytes 98308
  1.5 10.6 %collective-permute-start = (f32[128]{0:T(128)S(1)}, f32[128]{0:T(128)S(1)}, u32[]{:S(2)}, u32[]{:S(2)}) collective-permute-start(f32[128]{0:T(128)S(1)} %slice_bitcast_fusion), channel_id=1, source_target_pairs={{64,0},{128,64},{192,128},{65,1},{129,65},{193,129},{66,2},{130,66... | collective-permute-start | bytes 1544 | tf_op jit(solution)/shard_map/ppermute | solution.py:17
  6.2 15.5 %collective-permute-start.1 = (f32[10,4,128]{2,1,0:T(4,128)}, f32[10,4,128]{2,1,0:T(4,128)}, u32[]{:S(2)}, u32[]{:S(2)}) collective-permute-start(f32[10,4,128]{2,1,0:T(4,128)} %bitcast.2), channel_id=1, source_target_pairs={{64,0},{128,64},{192,128},{65,1},{129,65},{193,129},{66,2},{130,66... | collective-permute-start | bytes 61448 | tf_op jit(solution)/shard_map/ppermute | solution.py:17
  12.1 0.6 copy-start.5
  18.1 3.6 %copy-start.2 = (f32[10,4,64,128]{3,2,1,0:T(8,128)S(1)}, f32[10,4,64,128]{3,2,1,0:T(8,128)}, u32[]{:S(2)}) copy-start(f32[10,4,64,128]{3,2,1,0:T(8,128)} %param.6) | copy-start | bytes 3932164
  35.2 5.6 %copy-start.1 = (f32[10,10,4,64]{0,1,3,2:T(8,128)S(1)}, f32[10,10,4,64]{0,1,3,2:T(8,128)}, u32[]{:S(2)}) copy-start(f32[10,10,4,64]{0,1,3,2:T(8,128)} %fusion.10) | copy-start | bytes 307204
  72.8 17.3 %copy-start.4 = (f32[64,128]{1,0:T(8,128)S(1)}, f32[64,128]{1,0:T(8,128)}, u32[]{:S(2)}) copy-start(f32[64,128]{1,0:T(8,128)} %copy-done.3) | copy-start | bytes 98308
  72.8 17.3 %copy-start.6 = (f32[64,128]{1,0:T(8,128)S(1)}, f32[64,128]{1,0:T(8,128)}, u32[]{:S(2)}) copy-start(f32[64,128]{1,0:T(8,128)} %copy-done.5) | copy-start | bytes 98308
  72.8 17.3 %copy-start.7 = (s32[64,128]{1,0:T(8,128)S(1)}, s32[64,128]{1,0:T(8,128)}, u32[]{:S(2)}) copy-start(s32[64,128]{1,0:T(8,128)} %param.9) | copy-start | bytes 98308
  77.0 13.1 %all-to-all-start.1 = ((f32[64,10,4,1]{1,2,3,0:T(4,128)}), f32[64,10,4,1]{1,2,3,0:T(4,128)S(1)}, u32[]{:S(2)}, u32[]{:S(2)}) async-start(f32[64,10,4,1]{1,2,3,0:T(4,128)} %broadcast_in_dim.11), calls=%async_computation.1 | async-start | bytes 262144 | tf_op jit(solution)/shard_map/all_to_all | solution.py:48
where the time goes:
time: 91.9 us; the launch traced here: 91.2 us
  local copies, waits for them, and re-layouts  27.8 us (30%)
  blocking collectives  19.2 us (21%)
  matrix products  18.1 us (20%)
  starting transfers between devices  10.1 us (11%)
  waiting for transfers between devices  7.99 us (9%)
  other arithmetic  7.14 us (8%)
    all_to_all x1, blocking collectives, sum_at_owner(): blocks = lax.all_to_all(cut_along(x, dim, count), axis, 0, 0, tiled=True)  19.2 us
    all_to_all x1, waiting for transfers between devices, copy_for_each(): lax.all_to_all(jnp.broadcast_to(x[None], (count, *x.shape)), axis, 0, 0,...  7.98 us
    concatenate x1, local copies, waits for them, and re-layouts, side_by_side(): both = jnp.concatenate(arrays, axis=along)  7.68 us
    ppermute x2, starting transfers between devices, shifted(): return lax.ppermute(block, axis, route)  5.58 us
    dot_general x1, matrix products, shards(): jnp.einsum('yalq,falq->fyal', scaling_factors, warmth_entry, precision=hi...  5.41 us
    dot_general x1, matrix products, shards(): jnp.einsum('yalq,falq->fyal', scaling_factors, poleward_flow, precision=h...  5.32 us
    unnamed x22, local copies, waits for them, and re-layouts  4.59 us
    all_to_all x1, starting transfers between devices, copy_for_each(): lax.all_to_all(jnp.broadcast_to(x[None], (count, *x.shape)), axis, 0, 0,...  4.52 us
  transfers between devices with their start and end apart: 3, of which 1 were waited for; matrix products, arithmetic and copies ran while one was open for 16% of the time, Pallas kernels for 0%

commit v1 on v0

v1 whole, which is shorter than its diff:
```python
import functools
import math

import jax
import jax.numpy as jnp
from jax import lax
from jax.experimental import pallas as pl
from jax.experimental.pallas import tpu as pltpu
from jax.sharding import PartitionSpec as P

BASINS = 10
GROUP = 16
SUB = 8
LANES = 128
MESH = pl.DeviceIdType.MESH


def kernel(
    dims,
    flow_hbm,
    warmth_hbm,
    flag_hbm,
    floor_hbm,
    label_hbm,
    eddy_ref,
    transport_ref,
    flow,
    warmth,
    flag,
    floor,
    label,
    depth,
    limit,
    mean_warmth,
    split,
    edge,
    edge_in,
    tiles,
    tiles_in,
    bar,
    bar_in,
    flow_sem,
    warmth_sem,
    small_sem,
    edge_send,
    edge_recv,
    tile_send,
    tile_recv,
    bar_send,
    bar_recv,
):
    times, levels, rows, pitch, lats, lons, scaling = dims
    steps = rows // SUB
    lat, lon = lax.axis_index("lat"), lax.axis_index("lon")
    fields = times * levels
    flat_warmth = warmth.reshape(fields * pitch, LANES)

    def flow_copy(n):
        part = pl.ds(pl.multiple_of(n * SUB, SUB), SUB)
        return pltpu.make_async_copy(flow_hbm.at[:, part], flow.at[:, part], flow_sem.at[n])

    def warmth_copy(n):
        part = pl.ds(pl.multiple_of(n * SUB, SUB), SUB)
        return pltpu.make_async_copy(warmth_hbm.at[:, part], warmth.at[:, part], warmth_sem.at[n])

    smalls = [
        pltpu.make_async_copy(flag_hbm, flag, small_sem.at[0]),
        pltpu.make_async_copy(floor_hbm, floor, small_sem.at[1]),
        pltpu.make_async_copy(label_hbm, label, small_sem.at[2]),
    ]
    warmth_copy(0).start()
    for copy in smalls:
        copy.start()
    for n in range(steps):
        if n:
            warmth_copy(n).start()
        flow_copy(n).start()

    barrier = pltpu.get_barrier_semaphore()

    def greet(i, _):
        peer = lax.rem(lon + i, lons)
        pl.semaphore_signal(barrier, inc=1, device_id=(lat, peer), device_id_type=MESH)
        return 0

    lax.fori_loop(1, lons, greet, 0)

    @pl.when(lat < lats - 1)
    def _():
        pl.semaphore_signal(barrier, inc=1, device_id=(lat + 1, lon), device_id_type=MESH)

    for copy in smalls:
        copy.wait()
    warmth_copy(0).wait()
    depth[0:rows, :] = flag[...] * floor[...]
    for a in range(fields // SUB):
        edge[a * SUB : (a + 1) * SUB, :] = flat_warmth[pl.ds(a * SUB * pitch, SUB, stride=pitch), :]
    edge[fields : fields + SUB, :] = depth[0:SUB, :].astype(jnp.float32)
    tiles_in[pl.ds(pl.multiple_of(lon * SUB, SUB), SUB), :] = jnp.zeros((SUB, LANES), jnp.float32)

    edge_copy = pltpu.make_async_remote_copy(
        src_ref=edge,
        dst_ref=edge_in,
        send_sem=edge_send,
        recv_sem=edge_recv,
        device_id=(lat - 1, lon),
        device_id_type=MESH,
    )
    pl.semaphore_wait(barrier, jnp.where(lat > 0, lons, lons - 1))

    @pl.when(lat > 0)
    def _():
        edge_copy.start()

    lane = lax.broadcasted_iota(jnp.int32, (SUB, LANES), 1)
    sub = lax.broadcasted_iota(jnp.int32, (SUB, LANES), 0)

    def step(n):
        row = pl.multiple_of(n * SUB, SUB)
        here = pl.ds(row, SUB)
        next_depth = depth[pl.ds(row + 1, SUB), :]
        lim = jnp.minimum(depth[here, :], next_depth)
        limit[here, :] = lim
        for k in range(levels):
            wet = jnp.where(lim > k, 1.0, 0.0)
            v = [flow[t * levels + k, here, :] for t in range(times)]
            w = [
                0.5
                * (
                    warmth[t * levels + k, here, :]
                    + flat_warmth[pl.ds((t * levels + k) * pitch + row + 1, SUB), :]
                )
                for t in range(times)
            ]
            mean_v = functools.reduce(jnp.add, v) * (1.0 / times)
            mean_w = functools.reduce(jnp.add, w) * (1.0 / times)
            mean_warmth[k, here, :] = mean_w
            cross = functools.reduce(
                jnp.add, [(v[t] - mean_v) * (w[t] - mean_w) for t in range(times)]
            ) * (1.0 / times)
            chunks = [x * wet for x in v] + [x * wet for x in w]
            chunks += [wet, mean_v * mean_w * wet, cross * wet, jnp.zeros_like(wet)]
            for c in range(0, len(chunks), 2):
                both = jnp.concatenate(chunks[c : c + 2], axis=0)
                high = both.astype(jnp.bfloat16)
                low = (both - high.astype(jnp.float32)).astype(jnp.bfloat16)
                at = (k * len(chunks) + c) * SUB
                split[at : at + 2 * SUB, 0:LANES] = high
                split[at : at + 2 * SUB, LANES : 2 * LANES] = low
        iota = lax.broadcasted_iota(jnp.int32, (GROUP, LANES), 0)
        tags = label[here, :]
        hot = jnp.concatenate(
            [
                jnp.where(
                    jnp.broadcast_to(tags[r : r + 1, :], (GROUP, LANES)) == iota,
                    1.0,
                    0.0,
                )
                for r in (0, *range(SUB - 1, 0, -1))
            ],
            axis=0,
        ).astype(jnp.bfloat16)
        hot = jnp.concatenate([hot, hot], axis=1)
        out = lax.dot_general(
            split[...], hot, (((1,), (1,)), ((), ())), preferred_element_type=jnp.float32
        )
        width = 2 * times + 4
        slots = times + 2

        def piece(k, c, m):
            x = out[(k * width + c) * SUB : (k * width + c + 1) * SUB, :]
            return pltpu.roll(x, 10 * m, axis=1) if m else x

        turned = (lane + GROUP * sub) % LANES
        marks = [(turned >= 10 * m) & (turned < 10 * m + 10) for m in range(slots)]
        for k in range(levels):
            count = piece(k, 2 * times, times)
            for half in range(2):
                acc = jnp.where(marks[times], count, 0.0)
                for t in range(times):
                    acc = jnp.where(marks[t], piece(k, half * times + t, t), acc)
                acc = jnp.where(marks[times + 1], piece(k, 2 * times + 1 + half, times + 1), acc)
                tiles[pl.ds(row * SUB + half * levels + k, SUB, stride=SUB), :] = pltpu.roll(
                    acc, 0, axis=1, stride=GROUP, stride_axis=0
                )

    def early(n, _):
        warmth_copy(n + 1).wait()
        flow_copy(n).wait()
        step(n)
        return 0

    lax.fori_loop(0, steps - 1, early, 0)
    flow_copy(steps - 1).wait()

    @pl.when(lat < lats - 1)
    def _():
        edge_copy.wait_recv()
        for a in range(fields // SUB):
            flat_warmth[pl.ds(a * SUB * pitch + rows, SUB, stride=pitch), :] = edge_in[
                a * SUB : (a + 1) * SUB, :
            ]
        depth[rows : rows + SUB, :] = edge_in[fields : fields + SUB, :].astype(jnp.int32)

    @pl.when(lat == lats - 1)
    def _():
        for a in range(fields // SUB):
            flat_warmth[pl.ds(a * SUB * pitch + rows, SUB, stride=pitch), :] = jnp.zeros(
                (SUB, LANES), jnp.float32
            )
        depth[rows : rows + SUB, :] = jnp.zeros((SUB, LANES), jnp.int32)

    step(steps - 1)

    mine = pl.ds(pl.multiple_of(lon * SUB, SUB), SUB)

    def send_tile(i, _):
        peer = lax.rem(lon + i, lons)
        pltpu.make_async_remote_copy(
            src_ref=tiles.at[pl.ds(pl.multiple_of(peer * SUB, SUB), SUB)],
            dst_ref=tiles_in.at[mine],
            send_sem=tile_send,
            recv_sem=tile_recv,
            device_id=(lat, peer),
            device_id_type=MESH,
        ).start()
        return 0

    lax.fori_loop(1, lons, send_tile, 0)
    others = pl.ds(0, (lons - 1) * SUB)
    all_tiles = pltpu.make_async_remote_copy(
        src_ref=tiles.at[others],
        dst_ref=tiles_in.at[others],
        send_sem=tile_send,
        recv_sem=tile_recv,
        device_id=(lat, lon),
        device_id_type=MESH,
    )
    all_tiles.wait_recv()
    parts = [tiles[mine, :]] + [tiles_in[SUB * p : SUB * p + SUB, :] for p in range(lons)]
    while len(parts) > 1:
        parts = [sum(parts[i : i + 2][1:], parts[i]) for i in range(0, len(parts), 2)]
    total = parts[0]

    def moved(x, lanes):
        return pltpu.roll(x, (-lanes) % LANES, axis=1)

    count = moved(total, 10 * times)
    first = lane < BASINS
    divisor = jnp.maximum(count, 1.0)
    sums = total
    for t in range(1, times):
        sums = sums + moved(total, 10 * t)
    bars = jnp.where(first, sums / divisor * (1.0 / times), 0.0)
    spread = pltpu.roll(bars, 0, axis=1, stride=10, stride_axis=0)
    for shift in (4, 2, 1):
        spread = spread + pltpu.roll(spread, shift, axis=0)
    bar[...] = spread[0:1, :]
    bar_in[pl.ds(lon, 1)] = spread[0:1, :].reshape(1, 1, LANES)

    def send_bar(i, _):
        peer = lax.rem(lon + i, lons)
        pltpu.make_async_remote_copy(
            src_ref=bar,
            dst_ref=bar_in.at[lon],
            send_sem=bar_send,
            recv_sem=bar_recv,
            device_id=(lat, peer),
            device_id_type=MESH,
        ).start()
        return 0

    lax.fori_loop(1, lons, send_bar, 0)

    def other_half(x):
        return pltpu.roll(x, levels, axis=0)

    bars_w = other_half(bars)
    flow_part = scaling * count * bars * bars_w
    swing = jnp.zeros_like(total)
    for t in range(times):
        dev = (moved(total, 10 * t) if t else total) / divisor - bars
        swing = swing + dev * other_half(dev)
    swing = scaling * count * (swing * (1.0 / times))
    both = moved(total, 10 * (times + 1))
    steady = scaling * both - flow_part
    transient = scaling * other_half(both) - swing
    for q, value in enumerate((flow_part, steady, swing, transient)):
        for k in range(levels):
            transport_ref[q, k] = value[k : k + 1, 0:BASINS]

    every_bar = pltpu.make_async_remote_copy(
        src_ref=bar_in.at[pl.ds(0, lons - 1)],
        dst_ref=bar_in.at[pl.ds(0, lons - 1)],
        send_sem=bar_send,
        recv_sem=bar_recv,
        device_id=(lat, lon),
        device_id_type=MESH,
    )
    every_bar.wait_recv()
    for n in range(steps):
        here = slice(n * SUB, (n + 1) * SUB)
        table = bar_in[here].reshape(SUB, LANES)
        lim = limit[here, :]
        tags = label[here, :]
        for k in range(levels):
            cell = jnp.take_along_axis(
                table, tags + (levels * 10 + k * 10), axis=1, mode="promise_in_bounds"
            )
            eddy_ref[k, here, :] = jnp.where(lim > k, mean_warmth[k, here, :] - cell, 0.0)

    all_tiles.wait_send()
    every_bar.wait_send()

    @pl.when(lat > 0)
    def _():
        edge_copy.wait_send()


def shards(lats, lons, flow, warmth, flag, floor, label):
    times, levels, rows, cols = flow.shape
    fields = times * levels
    pitch = rows + SUB
    scaling = 1.0 / math.sqrt(cols * lons)
    dims = (times, levels, rows, pitch, lats, lons, scaling)
    anywhere = pl.BlockSpec(memory_space=pl.ANY)
    local = pl.BlockSpec(memory_space=pltpu.VMEM)
    dma = pltpu.SemaphoreType.DMA
    f32 = jnp.float32
    eddy, transport = pl.pallas_call(
        functools.partial(kernel, dims),
        out_shape=(
            jax.ShapeDtypeStruct((levels, rows, cols), f32),
            jax.ShapeDtypeStruct((4, levels, 1, BASINS), f32),
        ),
        in_specs=[anywhere] * 5,
        out_specs=(local, local),
        scratch_shapes=[
            pltpu.VMEM((fields, rows, cols), f32),
            pltpu.VMEM((fields, pitch, cols), f32),
            pltpu.VMEM((rows, cols), jnp.int32),
            pltpu.VMEM((rows, cols), jnp.int32),
            pltpu.VMEM((rows, cols), jnp.int32),
            pltpu.VMEM((pitch, cols), jnp.int32),
            pltpu.VMEM((rows, cols), jnp.int32),
            pltpu.VMEM((levels, rows, cols), f32),
            pltpu.VMEM((levels * (2 * times + 4) * SUB, 2 * cols), jnp.bfloat16),
            pltpu.VMEM((fields + SUB, cols), f32),
            pltpu.VMEM((fields + SUB, cols), f32),
            pltpu.VMEM((rows * SUB, cols), f32),
            pltpu.VMEM((rows * SUB, cols), f32),
            pltpu.VMEM((1, cols), f32),
            pltpu.VMEM((rows, 1, cols), f32),
            dma((rows // SUB,)),
            dma((rows // SUB,)),
            dma((3,)),
            dma,
            dma,
            dma,
            dma,
            dma,
            dma,
        ],
        compiler_params=pltpu.CompilerParams(collective_id=0, has_side_effects=True),
    )(
        flow.reshape(fields, rows, cols),
        warmth.reshape(fields, rows, cols),
        flag,
        floor,
        label,
    )
    return eddy, jnp.transpose(transport, (0, 3, 1, 2))


def solution(mesh):
    return jax.shard_map(
        functools.partial(shards, mesh.shape["lat"], mesh.shape["lon"]),
        mesh=mesh,
        in_specs=(
            P(None, None, "lat", "lon"),
            P(None, None, "lat", "lon"),
            P("lat", "lon"),
            P("lat", "lon"),
            P("lat", "lon"),
        ),
        out_specs=(P(None, "lat", "lon"), P(None, None, None, ("lat", "lon"))),
        check_vma=False,
    )
```

time: 91.9 us -> 30 us (0.33)
  the two profiles are of different devices: /device:TPU:193 before, /device:TPU:1 now
where the time goes in v1:
time: 30 us; the launch traced here: 29.9 us
  Pallas kernels  26.4 us (88%)
  local copies, waits for them, and re-layouts  2.86 us (10%)
  between operations  0.64 us (2%)
    pallas_call x1, Pallas kernels, shards(): pl.pallas_call(functools.partial(kernel, dims), out_shape=(jax.ShapeDtype...  26.4 us
    unnamed x2, local copies, waits for them, and re-layouts  2.86 us

profile of v1, /device:TPU:1, one launch (start us, length us, event | category | flops | bytes accessed | tf_op | source)
XLA Modules:
  0.0 29.9 jit_solution(10875318968637050428)
XLA Ops:
  0.6 26.4 %shard_map.68 = (f32[4,64,128]{2,1,0:T(8,128)}, f32[4,4,1,10]{3,2,1,0:T(1,128)}) custom-call(f32[40,64,128]{2,1,0:T(8,128)} %bitcast.3, f32[40,64,128]{2,1,0:T(8,128)} %bitcast.4, s32[64,128]{1,0:T(8,128)} %flag_hbm.1, s32[64,128]{1,0:T(8,128)} %floor_hbm.1, s32[64,128]{1,0:T(8,128)} %label_hbm.1), custom_call_target="tpu_custom_call" | custom-call | tf_op jit(solution)/shard_map/pallas_call | solution.py:330
  27.0 1.6 %copy.9 = f32[4,64,128]{2,1,0:T(8,128)} copy(f32[4,64,128]{2,1,0:T(8,128)} %get-tuple-element.8) | data formatting | bytes 262144
  28.6 1.3 %copy.10 = f32[4,10,4,1]{1,3,2,0:T(1,128)} copy(f32[4,10,4,1]{1,3,2,0:T(1,128)} %bitcast.5) | data formatting | bytes 1280

commit v2 on v1

--- a/solution.py
+++ b/solution.py
@@ -1,4 +1,5 @@
 import functools
+import itertools
 import math
 
 import jax
@@ -9,6 +10,7 @@
 from jax.sharding import PartitionSpec as P
 
 BASINS = 10
+FAN = 4
 GROUP = 16
 SUB = 8
 LANES = 128
@@ -32,7 +34,8 @@
     depth,
     limit,
     mean_warmth,
-    split,
+    split_even,
+    split_odd,
     edge,
     edge_in,
     tiles,
@@ -48,11 +51,14 @@
     tile_recv,
     bar_send,
     bar_recv,
+    met_sem,
 ):
+    splits = (split_even, split_odd)
     times, levels, rows, pitch, lats, lons, scaling = dims
     steps = rows // SUB
     lat, lon = lax.axis_index("lat"), lax.axis_index("lon")
     fields = times * levels
+    places = round(math.log(lons, FAN))
     flat_warmth = warmth.reshape(fields * pitch, LANES)
 
     def flow_copy(n):
@@ -77,13 +83,23 @@
         flow_copy(n).start()
 
     barrier = pltpu.get_barrier_semaphore()
-
-    def greet(i, _):
-        peer = lax.rem(lon + i, lons)
-        pl.semaphore_signal(barrier, inc=1, device_id=(lat, peer), device_id_type=MESH)
-        return 0
-
-    lax.fori_loop(1, lons, greet, 0)
+    digits = [lon // FAN**d % FAN for d in range(places)]
+    turned_digits = [
+        [lax.rem(digits[d] + i, FAN) * FAN**d for i in range(FAN)] for d in range(places)
+    ]
+
+    def signal_line(semaphore, d):
+        rest = lon - turned_digits[d][0]
+        for i in range(1, FAN):
+            pl.semaphore_signal(
+                semaphore,
+                inc=1,
+                device_id=(lat, rest + turned_digits[d][i]),
+                device_id_type=MESH,
+            )
+
+    for d in range(places):
+        signal_line(barrier, d)
 
     @pl.when(lat < lats - 1)
     def _():
@@ -106,18 +122,22 @@
         device_id=(lat - 1, lon),
         device_id_type=MESH,
     )
-    pl.semaphore_wait(barrier, jnp.where(lat > 0, lons, lons - 1))
+    met = places * (FAN - 1)
+    pl.semaphore_wait(barrier, jnp.where(lat > 0, met + 1, met))
 
     @pl.when(lat > 0)
     def _():
         edge_copy.start()
 
+    signal_line(met_sem.at[1], 1)
+
     lane = lax.broadcasted_iota(jnp.int32, (SUB, LANES), 1)
     sub = lax.broadcasted_iota(jnp.int32, (SUB, LANES), 0)
 
-    def step(n):
-        row = pl.multiple_of(n * SUB, SUB)
+    def prepare(n):
+        row = n * SUB
         here = pl.ds(row, SUB)
+        split = splits[n % 2]
         next_depth = depth[pl.ds(row + 1, SUB), :]
         lim = jnp.minimum(depth[here, :], next_depth)
         limit[here, :] = lim
@@ -147,6 +167,10 @@
                 at = (k * len(chunks) + c) * SUB
                 split[at : at + 2 * SUB, 0:LANES] = high
                 split[at : at + 2 * SUB, LANES : 2 * LANES] = low
+    def contract(n):
+        row = n * SUB
+        here = pl.ds(row, SUB)
+        split = splits[n % 2]
         iota = lax.broadcasted_iota(jnp.int32, (GROUP, LANES), 0)
         tags = label[here, :]
         hot = jnp.concatenate(
@@ -184,13 +208,16 @@
                     acc, 0, axis=1, stride=GROUP, stride_axis=0
                 )
 
-    def early(n, _):
+    for n in range(steps - 1):
         warmth_copy(n + 1).wait()
         flow_copy(n).wait()
-        step(n)
-        return 0
-
-    lax.fori_loop(0, steps - 1, early, 0)
+        prepare(n)
+        if n:
+            contract(n - 1)
+        for d in range(2, places):
+            if n == 2 * d:
+                pl.semaphore_wait(met_sem.at[d - 1], FAN - 1)
+                signal_line(met_sem.at[d], d)
     flow_copy(steps - 1).wait()
 
     @pl.when(lat < lats - 1)
@@ -210,12 +237,21 @@
             )
         depth[rows : rows + SUB, :] = jnp.zeros((SUB, LANES), jnp.int32)
 
-    step(steps - 1)
+    prepare(steps - 1)
+    contract(steps - 2)
+    contract(steps - 1)
+    pl.semaphore_wait(met_sem.at[places - 1], FAN - 1)
 
     mine = pl.ds(pl.multiple_of(lon * SUB, SUB), SUB)
 
-    def send_tile(i, _):
-        peer = lax.rem(lon + i, lons)
+    def far_first():
+        ways = itertools.product(range(FAN), repeat=places)
+        hops = lambda way: sum(min(i, FAN - i) for i in way[1:]) + (way[0] > 0)
+        for way in sorted(ways, key=hops, reverse=True):
+            if any(way):
+                yield sum(turned_digits[d][way[d]] for d in range(places))
+
+    for peer in far_first():
         pltpu.make_async_remote_copy(
             src_ref=tiles.at[pl.ds(pl.multiple_of(peer * SUB, SUB), SUB)],
             dst_ref=tiles_in.at[mine],
@@ -224,9 +260,6 @@
             device_id=(lat, peer),
             device_id_type=MESH,
         ).start()
-        return 0
-
-    lax.fori_loop(1, lons, send_tile, 0)
     others = pl.ds(0, (lons - 1) * SUB)
     all_tiles = pltpu.make_async_remote_copy(
         src_ref=tiles.at[others],
@@ -258,8 +291,7 @@
     bar[...] = spread[0:1, :]
     bar_in[pl.ds(lon, 1)] = spread[0:1, :].reshape(1, 1, LANES)
 
-    def send_bar(i, _):
-        peer = lax.rem(lon + i, lons)
+    for peer in far_first():
         pltpu.make_async_remote_copy(
             src_ref=bar,
             dst_ref=bar_in.at[lon],
@@ -268,9 +300,6 @@
             device_id=(lat, peer),
             device_id_type=MESH,
         ).start()
-        return 0
-
-    lax.fori_loop(1, lons, send_bar, 0)
 
     def other_half(x):
         return pltpu.roll(x, levels, axis=0)
@@ -317,23 +346,33 @@
         edge_copy.wait_send()
 
 
+def write_out(eddy, transport, eddy_out, transport_out, sem):
+    copies = [
+        pltpu.make_async_copy(eddy, eddy_out, sem.at[0]),
+        pltpu.make_async_copy(transport, transport_out, sem.at[1]),
+    ]
+    for copy in copies:
+        copy.start()
+    for copy in copies:
+        copy.wait()
+
+
 def shards(lats, lons, flow, warmth, flag, floor, label):
     times, levels, rows, cols = flow.shape
     fields = times * levels
     pitch = rows + SUB
     scaling = 1.0 / math.sqrt(cols * lons)
     dims = (times, levels, rows, pitch, lats, lons, scaling)
-    anywhere = pl.BlockSpec(memory_space=pl.ANY)
     local = pl.BlockSpec(memory_space=pltpu.VMEM)
     dma = pltpu.SemaphoreType.DMA
     f32 = jnp.float32
     eddy, transport = pl.pallas_call(
         functools.partial(kernel, dims),
         out_shape=(
-            jax.ShapeDtypeStruct((levels, rows, cols), f32),
-            jax.ShapeDtypeStruct((4, levels, 1, BASINS), f32),
+            pltpu.VMEM((levels, rows, cols), f32),
+            pltpu.VMEM((4, levels, 1, BASINS), f32),
         ),
-        in_specs=[anywhere] * 5,
+        in_specs=[pl.BlockSpec(memory_space=pltpu.HBM)] * 5,
         out_specs=(local, local),
         scratch_shapes=[
             pltpu.VMEM((fields, rows, cols), f32),
@@ -345,6 +384,7 @@
             pltpu.VMEM((rows, cols), jnp.int32),
             pltpu.VMEM((levels, rows, cols), f32),
             pltpu.VMEM((levels * (2 * times + 4) * SUB, 2 * cols), jnp.bfloat16),
+            pltpu.VMEM((levels * (2 * times + 4) * SUB, 2 * cols), jnp.bfloat16),
             pltpu.VMEM((fields + SUB, cols), f32),
             pltpu.VMEM((fields + SUB, cols), f32),
             pltpu.VMEM((rows * SUB, cols), f32),
@@ -360,8 +400,11 @@
             dma,
             dma,
             dma,
+            pltpu.SemaphoreType.REGULAR((round(math.log(lons, FAN)),)),
         ],
-        compiler_params=pltpu.CompilerParams(collective_id=0, has_side_effects=True),
+        compiler_params=pltpu.CompilerParams(
+            collective_id=0, has_side_effects=True, vmem_limit_bytes=66879488
+        ),
     )(
         flow.reshape(fields, rows, cols),
         warmth.reshape(fields, rows, cols),
@@ -369,6 +412,14 @@
         floor,
         label,
     )
+    eddy, transport = pl.pallas_call(
+        write_out,
+        out_shape=tuple(jax.ShapeDtypeStruct(a.shape, a.dtype) for a in (eddy, transport)),
+        in_specs=[local] * 2,
+        out_specs=[pl.BlockSpec(memory_space=pltpu.HBM)] * 2,
+        scratch_shapes=[dma((2,))],
+        compiler_params=pltpu.CompilerParams(vmem_limit_bytes=2**20),
+    )(eddy, transport)
     return eddy, jnp.transpose(transport, (0, 3, 1, 2))
 
 

time: 30 us -> 23.8 us (0.79)
  Pallas kernels: 26.4 us -> 23 us
  local copies, waits for them, and re-layouts: 2.86 us -> 0 us
    pallas_call x1 -> x2, Pallas kernels: 26.4 us -> 23 us  [the longest x1 22.4 us: shards(): pl.pallas_call(functools.partial(kernel, dims), out_shape=(pltpu.VMEM((le...]
    unnamed x2 -> x0, local copies, waits for them, and re-layouts: 2.86 us -> none
where the time goes in v2:
time: 23.8 us; the launch traced here: 23.7 us
  Pallas kernels  23 us (97%)
  between operations  0.64 us (3%)
    pallas_call x1, Pallas kernels, shards(): pl.pallas_call(functools.partial(kernel, dims), out_shape=(pltpu.VMEM((le...  22.4 us
    pallas_call x1, Pallas kernels, shards(): pl.pallas_call(write_out, out_shape=tuple((jax.ShapeDtypeStruct(a.shape,...  0.68 us

profile of v2, /device:TPU:1, one launch (start us, length us, event | category | flops | bytes accessed | tf_op | source)
XLA Modules:
  0.0 23.7 jit_solution(17873568326733752676)
XLA Ops:
  0.6 22.4 %shard_map.68 = (f32[4,64,128]{2,1,0:T(8,128)S(1)}, f32[4,4,1,10]{3,2,1,0:T(1,128)S(1)}) custom-call(f32[40,64,128]{2,1,0:T(8,128)} %bitcast.3, f32[40,64,128]{2,1,0:T(8,128)} %bitcast.4, s32[64,128]{1,0:T(8,128)} %flag_hbm.1, s32[64,128]{1,0:T(8,128)} %floor_hbm.1, s32[64,128]{1,0:T(8,128)} %label_hbm.1), custom_call_target="tpu_custom_call" | custom-call | tf_op jit(solution)/shard_map/pallas_call | solution.py:369
  23.0 0.7 %shard_map.69 = (f32[4,64,128]{2,1,0:T(8,128)}, f32[4,4,1,10]{3,2,1,0:T(1,128)}) custom-call(f32[4,64,128]{2,1,0:T(8,128)S(1)} %get-tuple-element.6.eddy, f32[4,4,1,10]{3,2,1,0:T(1,128)S(1)} %get-tuple-element.7.transport), custom_call_target="tpu_custom_call" | custom-call | tf_op jit(solution)/shard_map/pallas_call | solution.py:415

commit v3 on v2

--- a/solution.py
+++ b/solution.py
@@ -42,6 +42,10 @@
     tiles_in,
     bar,
     bar_in,
+    edge_line,
+    edge_lines,
+    lines,
+    lines_in,
     flow_sem,
     warmth_sem,
     small_sem,
@@ -51,6 +55,10 @@
     tile_recv,
     bar_send,
     bar_recv,
+    line_send,
+    line_recv,
+    edge_line_send,
+    edge_line_recv,
     met_sem,
 ):
     splits = (split_even, split_odd)
@@ -58,7 +66,11 @@
     steps = rows // SUB
     lat, lon = lax.axis_index("lat"), lax.axis_index("lon")
     fields = times * levels
+    last = rows - 1
+    mine = pl.ds(pl.multiple_of(lon * SUB, SUB), SUB)
     places = round(math.log(lons, FAN))
+    flat_flow = flow.reshape(fields * rows, LANES)
+    flat_mean = mean_warmth.reshape(levels * rows, LANES)
     flat_warmth = warmth.reshape(fields * pitch, LANES)
 
     def flow_copy(n):
@@ -77,34 +89,41 @@
     warmth_copy(0).start()
     for copy in smalls:
         copy.start()
+
+    barrier = pltpu.get_barrier_semaphore()
+    turned_digits = [
+        [lax.rem(lon // FAN**d + i, FAN) * FAN**d for i in range(FAN)] for d in range(places)
+    ]
+
+    def far_first():
+        ways = itertools.product(range(FAN), repeat=places)
+        hops = lambda way: sum(min(i, FAN - i) for i in way[1:]) + (way[0] > 0)
+        return [way for way in sorted(ways, key=hops, reverse=True) if any(way)]
+
+    def at(way):
+        return sum(turned_digits[d][way[d]] for d in range(places))
+
+    def across(way):
+        return way[1] > 0 and not any(way[:1] + way[2:])
+
+    greeted = [way for way in far_first() if across(way) or way[1] == 0]
+    for way in greeted:
+        pl.semaphore_signal(barrier, inc=1, device_id=(lat, at(way)), device_id_type=MESH)
+
+    @pl.when(lat < lats - 1)
+    def _():
+        pl.semaphore_signal(barrier, inc=1, device_id=(lat + 1, lon), device_id_type=MESH)
+
     for n in range(steps):
         if n:
             warmth_copy(n).start()
         flow_copy(n).start()
-
-    barrier = pltpu.get_barrier_semaphore()
-    digits = [lon // FAN**d % FAN for d in range(places)]
-    turned_digits = [
-        [lax.rem(digits[d] + i, FAN) * FAN**d for i in range(FAN)] for d in range(places)
-    ]
-
-    def signal_line(semaphore, d):
-        rest = lon - turned_digits[d][0]
-        for i in range(1, FAN):
-            pl.semaphore_signal(
-                semaphore,
-                inc=1,
-                device_id=(lat, rest + turned_digits[d][i]),
-                device_id_type=MESH,
-            )
-
-    for d in range(places):
-        signal_line(barrier, d)
-
-    @pl.when(lat < lats - 1)
-    def _():
-        pl.semaphore_signal(barrier, inc=1, device_id=(lat + 1, lon), device_id_type=MESH)
-
+    for a in range(fields // SUB):
+        flat_warmth[pl.ds(a * SUB * pitch + rows, SUB, stride=pitch), :] = jnp.zeros(
+            (SUB, LANES), jnp.float32
+        )
+    depth[rows : rows + SUB, :] = jnp.zeros((SUB, LANES), jnp.int32)
+    tiles_in[mine, :] = jnp.zeros((SUB, LANES), jnp.float32)
     for copy in smalls:
         copy.wait()
     warmth_copy(0).wait()
@@ -112,7 +131,6 @@
     for a in range(fields // SUB):
         edge[a * SUB : (a + 1) * SUB, :] = flat_warmth[pl.ds(a * SUB * pitch, SUB, stride=pitch), :]
     edge[fields : fields + SUB, :] = depth[0:SUB, :].astype(jnp.float32)
-    tiles_in[pl.ds(pl.multiple_of(lon * SUB, SUB), SUB), :] = jnp.zeros((SUB, LANES), jnp.float32)
 
     edge_copy = pltpu.make_async_remote_copy(
         src_ref=edge,
@@ -122,14 +140,16 @@
         device_id=(lat - 1, lon),
         device_id_type=MESH,
     )
-    met = places * (FAN - 1)
+    met = len(greeted)
     pl.semaphore_wait(barrier, jnp.where(lat > 0, met + 1, met))
 
     @pl.when(lat > 0)
     def _():
         edge_copy.start()
 
-    signal_line(met_sem.at[1], 1)
+    for way in greeted:
+        if across(way):
+            pl.semaphore_signal(met_sem, inc=1, device_id=(lat, at(way)), device_id_type=MESH)
 
     lane = lax.broadcasted_iota(jnp.int32, (SUB, LANES), 1)
     sub = lax.broadcasted_iota(jnp.int32, (SUB, LANES), 0)
@@ -159,7 +179,7 @@
                 jnp.add, [(v[t] - mean_v) * (w[t] - mean_w) for t in range(times)]
             ) * (1.0 / times)
             chunks = [x * wet for x in v] + [x * wet for x in w]
-            chunks += [wet, mean_v * mean_w * wet, cross * wet, jnp.zeros_like(wet)]
+            chunks += [wet, mean_v * mean_w * wet, cross * wet, mean_w * wet]
             for c in range(0, len(chunks), 2):
                 both = jnp.concatenate(chunks[c : c + 2], axis=0)
                 high = both.astype(jnp.bfloat16)
@@ -197,6 +217,12 @@
 
         turned = (lane + GROUP * sub) % LANES
         marks = [(turned >= 10 * m) & (turned < 10 * m + 10) for m in range(slots)]
+        line = jnp.zeros_like(lane, jnp.float32)
+        for k in range(levels):
+            line = jnp.where(marks[k], piece(k, 2 * times, k), line)
+            line = jnp.where(marks[levels + k], piece(k, width - 1, levels + k), line)
+        line = pltpu.roll(line, 0, axis=1, stride=GROUP, stride_axis=0)
+        lines[here] = line.reshape(SUB, 1, LANES)
         for k in range(levels):
             count = piece(k, 2 * times, times)
             for half in range(2):
@@ -208,68 +234,163 @@
                     acc, 0, axis=1, stride=GROUP, stride_axis=0
                 )
 
-    for n in range(steps - 1):
-        warmth_copy(n + 1).wait()
-        flow_copy(n).wait()
-        prepare(n)
-        if n:
-            contract(n - 1)
-        for d in range(2, places):
-            if n == 2 * d:
-                pl.semaphore_wait(met_sem.at[d - 1], FAN - 1)
-                signal_line(met_sem.at[d], d)
-    flow_copy(steps - 1).wait()
-
-    @pl.when(lat < lats - 1)
-    def _():
-        edge_copy.wait_recv()
-        for a in range(fields // SUB):
-            flat_warmth[pl.ds(a * SUB * pitch + rows, SUB, stride=pitch), :] = edge_in[
-                a * SUB : (a + 1) * SUB, :
-            ]
-        depth[rows : rows + SUB, :] = edge_in[fields : fields + SUB, :].astype(jnp.int32)
-
-    @pl.when(lat == lats - 1)
-    def _():
-        for a in range(fields // SUB):
-            flat_warmth[pl.ds(a * SUB * pitch + rows, SUB, stride=pitch), :] = jnp.zeros(
-                (SUB, LANES), jnp.float32
-            )
-        depth[rows : rows + SUB, :] = jnp.zeros((SUB, LANES), jnp.int32)
-
-    prepare(steps - 1)
-    contract(steps - 2)
+    def edge_sums():
+        lim = jnp.minimum(
+            depth[last : last + 1, :], edge_in[fields : fields + 1, :].astype(jnp.int32)
+        )
+        limit[last : last + 1, :] = lim
+        wet = jnp.where(jnp.broadcast_to(lim, (SUB, LANES)) > sub % levels, 1.0, 0.0)
+        x = []
+        for t in range(times):
+            v = flat_flow[pl.ds(t * levels * rows + last, levels, stride=rows), :]
+            w = flat_warmth[pl.ds(t * levels * pitch + last, levels, stride=pitch), :]
+            w = 0.5 * (w + edge_in[t * levels : (t + 1) * levels, :])
+            x.append(jnp.concatenate([v, w], axis=0))
+        mean = functools.reduce(jnp.add, x) * (1.0 / times)
+        flat_mean[pl.ds(last, levels, stride=rows), :] = mean[levels:, :]
+        devs = [y - mean for y in x]
+        cross = functools.reduce(jnp.add, [y * other_half(y) for y in devs]) * (1.0 / times)
+        both = jnp.where(sub < levels, mean * other_half(mean), cross)
+        chunks = jnp.concatenate([y * wet for y in x] + [wet, both * wet], axis=0)
+        high = chunks.astype(jnp.bfloat16)
+        low = (chunks - high.astype(jnp.float32)).astype(jnp.bfloat16)
+        iota = lax.broadcasted_iota(jnp.int32, (LANES, LANES), 0)
+        tags = jnp.broadcast_to(label[last : last + 1, :], (LANES, LANES))
+        hot = jnp.where(tags == iota, 1.0, 0.0).astype(jnp.bfloat16)
+        out = lax.dot_general(
+            jnp.concatenate([high, low], axis=1),
+            jnp.concatenate([hot, hot], axis=1),
+            (((1,), (1,)), ((), ())),
+            preferred_element_type=jnp.float32,
+        )
+        out = [out[m * SUB : (m + 1) * SUB, :] for m in range(times + 2)]
+        tiles[last * SUB : (last + 1) * SUB, :] = functools.reduce(
+            jnp.add, [pltpu.roll(y, BASINS * m, axis=1) if m else y for m, y in enumerate(out)]
+        )
+        total = functools.reduce(jnp.add, out[:times])
+        return in_one_row(jnp.where(sub < levels, out[times], total))
+
+    def other_half(x):
+        return pltpu.roll(x, levels, axis=0)
+
+    def over_sublanes(x):
+        for shift in (4, 2, 1):
+            x = x + pltpu.roll(x, shift, axis=0)
+        return x
+
+    def in_one_row(x):
+        return over_sublanes(pltpu.roll(x, 0, axis=1, stride=BASINS, stride_axis=0))[0:1, :]
+
+    cuts = (0, steps // 2, steps)
+    for low_cut, high_cut in itertools.pairwise(cuts):
+        for n in range(low_cut, high_cut):
+            if n + 1 < steps:
+                warmth_copy(n + 1).wait()
+            flow_copy(n).wait()
+        for n in range(low_cut, high_cut):
+            prepare(n)
+            if n:
+                contract(n - 1)
     contract(steps - 1)
-    pl.semaphore_wait(met_sem.at[places - 1], FAN - 1)
-
-    mine = pl.ds(pl.multiple_of(lon * SUB, SUB), SUB)
-
-    def far_first():
-        ways = itertools.product(range(FAN), repeat=places)
-        hops = lambda way: sum(min(i, FAN - i) for i in way[1:]) + (way[0] > 0)
-        for way in sorted(ways, key=hops, reverse=True):
-            if any(way):
-                yield sum(turned_digits[d][way[d]] for d in range(places))
-
-    for peer in far_first():
-        pltpu.make_async_remote_copy(
+    pl.semaphore_wait(met_sem, FAN - 1)
+
+    def tile_copy(peer):
+        return pltpu.make_async_remote_copy(
             src_ref=tiles.at[pl.ds(pl.multiple_of(peer * SUB, SUB), SUB)],
             dst_ref=tiles_in.at[mine],
             send_sem=tile_send,
             recv_sem=tile_recv,
             device_id=(lat, peer),
             device_id_type=MESH,
+        )
+
+    def line_copy(peer):
+        return pltpu.make_async_remote_copy(
+            src_ref=lines.at[peer],
+            dst_ref=lines_in.at[lon],
+            send_sem=line_send,
+            recv_sem=line_recv,
+            device_id=(lat, peer),
+            device_id_type=MESH,
+        )
+
+    lines_in[pl.ds(lon, 1)] = lines[pl.ds(lon, 1)]
+    for copy in (line_copy, tile_copy):
+        for peer in map(at, far_first()):
+
+            @pl.when(peer != last)
+            def _():
+                copy(peer).start()
+
+    @pl.when(lat < lats - 1)
+    def _():
+        edge_copy.wait_recv()
+
+    @pl.when(lat == lats - 1)
+    def _():
+        edge_in[...] = jnp.zeros_like(edge_in)
+
+    line = edge_sums()
+    edge_line[...] = line
+    edge_lines[pl.ds(lon, 1)] = line.reshape(1, 1, LANES)
+    for peer in map(at, far_first()):
+        pltpu.make_async_remote_copy(
+            src_ref=edge_line,
+            dst_ref=edge_lines.at[lon],
+            send_sem=edge_line_send,
+            recv_sem=edge_line_recv,
+            device_id=(lat, peer),
+            device_id_type=MESH,
         ).start()
-    others = pl.ds(0, (lons - 1) * SUB)
-    all_tiles = pltpu.make_async_remote_copy(
-        src_ref=tiles.at[others],
-        dst_ref=tiles_in.at[others],
-        send_sem=tile_send,
-        recv_sem=tile_recv,
-        device_id=(lat, lon),
-        device_id_type=MESH,
-    )
-    all_tiles.wait_recv()
+
+    @pl.when(lon != last)
+    def _():
+        tile_copy(last).start()
+
+    def wait_for(ref, count, send_sem, recv_sem):
+        part = pl.ds(0, count)
+        return pltpu.make_async_remote_copy(
+            src_ref=ref.at[part],
+            dst_ref=ref.at[part],
+            send_sem=send_sem,
+            recv_sem=recv_sem,
+            device_id=(lat, lon),
+            device_id_type=MESH,
+        )
+
+    every_line = wait_for(lines_in, lons - 1, line_send, line_recv)
+    fewer_lines = wait_for(lines_in, lons - 2, line_send, line_recv)
+    every_edge_line = wait_for(edge_lines, lons - 1, edge_line_send, edge_line_recv)
+    every_bar = wait_for(bar_in, lons - 1, bar_send, bar_recv)
+    fewer_bars = wait_for(bar_in, lons - 2, bar_send, bar_recv)
+    every_tile = wait_for(tiles_in, (lons - 1) * SUB, tile_send, tile_recv)
+
+    def summed(ref):
+        total = ref[0:SUB].reshape(SUB, LANES)
+        for n in range(1, lons // SUB):
+            total = total + ref[n * SUB : (n + 1) * SUB].reshape(SUB, LANES)
+        return over_sublanes(total)
+
+    def ratio(total):
+        return total / jnp.maximum(pltpu.roll(total, levels * BASINS, axis=1), 1.0)
+
+    @pl.when(lon != last)
+    def _():
+        every_line.wait_recv()
+        line = ratio(summed(lines_in))[0:1, :]
+        bar[...] = line
+        bar_in[pl.ds(lon, 1)] = line.reshape(1, 1, LANES)
+        for peer in map(at, far_first()):
+            pltpu.make_async_remote_copy(
+                src_ref=bar,
+                dst_ref=bar_in.at[lon],
+                send_sem=bar_send,
+                recv_sem=bar_recv,
+                device_id=(lat, peer),
+                device_id_type=MESH,
+            ).start()
+
+    every_tile.wait_recv()
     parts = [tiles[mine, :]] + [tiles_in[SUB * p : SUB * p + SUB, :] for p in range(lons)]
     while len(parts) > 1:
         parts = [sum(parts[i : i + 2][1:], parts[i]) for i in range(0, len(parts), 2)]
@@ -285,25 +406,6 @@
     for t in range(1, times):
         sums = sums + moved(total, 10 * t)
     bars = jnp.where(first, sums / divisor * (1.0 / times), 0.0)
-    spread = pltpu.roll(bars, 0, axis=1, stride=10, stride_axis=0)
-    for shift in (4, 2, 1):
-        spread = spread + pltpu.roll(spread, shift, axis=0)
-    bar[...] = spread[0:1, :]
-    bar_in[pl.ds(lon, 1)] = spread[0:1, :].reshape(1, 1, LANES)
-
-    for peer in far_first():
-        pltpu.make_async_remote_copy(
-            src_ref=bar,
-            dst_ref=bar_in.at[lon],
-            send_sem=bar_send,
-            recv_sem=bar_recv,
-            device_id=(lat, peer),
-            device_id_type=MESH,
-        ).start()
-
-    def other_half(x):
-        return pltpu.roll(x, levels, axis=0)
-
     bars_w = other_half(bars)
     flow_part = scaling * count * bars * bars_w
     swing = jnp.zeros_like(total)
@@ -318,18 +420,21 @@
         for k in range(levels):
             transport_ref[q, k] = value[k : k + 1, 0:BASINS]
 
-    every_bar = pltpu.make_async_remote_copy(
-        src_ref=bar_in.at[pl.ds(0, lons - 1)],
-        dst_ref=bar_in.at[pl.ds(0, lons - 1)],
-        send_sem=bar_send,
-        recv_sem=bar_recv,
-        device_id=(lat, lon),
-        device_id_type=MESH,
-    )
-    every_bar.wait_recv()
+    every_edge_line.wait_recv()
+    last_bars = ratio(summed(edge_lines)) * (1.0 / times)
+    @pl.when(lon != last)
+    def _():
+        fewer_bars.wait_recv()
+
+    @pl.when(lon == last)
+    def _():
+        every_bar.wait_recv()
+
     for n in range(steps):
         here = slice(n * SUB, (n + 1) * SUB)
         table = bar_in[here].reshape(SUB, LANES)
+        if n == steps - 1:
+            table = jnp.where(sub == SUB - 1, last_bars, table)
         lim = limit[here, :]
         tags = label[here, :]
         for k in range(levels):
@@ -338,8 +443,17 @@
             )
             eddy_ref[k, here, :] = jnp.where(lim > k, mean_warmth[k, here, :] - cell, 0.0)
 
-    all_tiles.wait_send()
-    every_bar.wait_send()
+    every_tile.wait_send()
+    every_edge_line.wait_send()
+
+    @pl.when(lon != last)
+    def _():
+        fewer_lines.wait_send()
+        every_bar.wait_send()
+
+    @pl.when(lon == last)
+    def _():
+        every_line.wait_send()
 
     @pl.when(lat > 0)
     def _():
@@ -391,6 +505,10 @@
             pltpu.VMEM((rows * SUB, cols), f32),
             pltpu.VMEM((1, cols), f32),
             pltpu.VMEM((rows, 1, cols), f32),
+            pltpu.VMEM((1, cols), f32),
+            pltpu.VMEM((rows, 1, cols), f32),
+            pltpu.VMEM((rows, 1, cols), f32),
+            pltpu.VMEM((rows, 1, cols), f32),
             dma((rows // SUB,)),
             dma((rows // SUB,)),
             dma((3,)),
@@ -400,7 +518,11 @@
             dma,
             dma,
             dma,
-            pltpu.SemaphoreType.REGULAR((round(math.log(lons, FAN)),)),
+            dma,
+            dma,
+            dma,
+            dma,
+            pltpu.SemaphoreType.REGULAR,
         ],
         compiler_params=pltpu.CompilerParams(
             collective_id=0, has_side_effects=True, vmem_limit_bytes=66879488

time: 23.8 us -> 20.7 us (0.87)
  Pallas kernels: 23 us -> 19.9 us
    pallas_call x1, Pallas kernels: 22.4 us -> 19.2 us  [shards(): pl.pallas_call(functools.partial(kernel, dims), out_shape=(pltpu.VMEM((le...]
where the time goes in v3:
time: 20.7 us; the launch traced here: 20.5 us
  Pallas kernels  19.9 us (96%)
  between operations  0.64 us (3%)
    pallas_call x1, Pallas kernels, shards(): pl.pallas_call(functools.partial(kernel, dims), out_shape=(pltpu.VMEM((le...  19.2 us
    pallas_call x1, Pallas kernels, shards(): pl.pallas_call(write_out, out_shape=tuple((jax.ShapeDtypeStruct(a.shape,...  0.68 us

profile of v3, /device:TPU:1, one launch (start us, length us, event | category | flops | bytes accessed | tf_op | source)
XLA Modules:
  0.0 20.5 jit_solution(12273348981462528115)
XLA Ops:
  0.6 19.2 %shard_map.68 = (f32[4,64,128]{2,1,0:T(8,128)S(1)}, f32[4,4,1,10]{3,2,1,0:T(1,128)S(1)}) custom-call(f32[40,64,128]{2,1,0:T(8,128)} %bitcast.3, f32[40,64,128]{2,1,0:T(8,128)} %bitcast.4, s32[64,128]{1,0:T(8,128)} %flag_hbm.1, s32[64,128]{1,0:T(8,128)} %floor_hbm.1, s32[64,128]{1,0:T(8,128)} %label_hbm.1), custom_call_target="tpu_custom_call" | custom-call | tf_op jit(solution)/shard_map/pallas_call | solution.py:483
  19.9 0.7 %shard_map.69 = (f32[4,64,128]{2,1,0:T(8,128)}, f32[4,4,1,10]{3,2,1,0:T(1,128)}) custom-call(f32[4,64,128]{2,1,0:T(8,128)S(1)} %get-tuple-element.6.eddy, f32[4,4,1,10]{3,2,1,0:T(1,128)S(1)} %get-tuple-element.7.transport), custom_call_target="tpu_custom_call" | custom-call | tf_op jit(solution)/shard_map/pallas_call | solution.py:537

commit v4 on v3

v4 whole, which is shorter than its diff:
```python
import functools
import itertools
import math

import jax
import jax.numpy as jnp
from jax import lax
from jax.experimental import pallas as pl
from jax.experimental.pallas import tpu as pltpu
from jax.sharding import PartitionSpec as P

BASINS = 10
OWNER_PART = 4
CORES = 2
FAN = 4
GROUP = 16
SUB = 8
LANES = 128
MESH = pl.DeviceIdType.MESH


def kernel(
    dims,
    flow_hbm,
    warmth_hbm,
    flag_hbm,
    floor_hbm,
    label_hbm,
    eddy_ref,
    transport_ref,
    flow,
    warmth,
    flag,
    floor,
    label,
    depth,
    limit,
    mean_warmth,
    sums,
    split_even,
    split_odd,
    edge,
    edge_in,
    edge_sum,
    edge_sum_in,
    tiles,
    tiles_in,
    bar,
    bar_in,
    edge_line,
    edge_lines,
    lines,
    lines_in,
    tiles_near,
    tiles_last,
    last_tile,
    own_total,
    flow_sem,
    warmth_sem,
    small_sem,
    edge_send,
    edge_recv,
    edge_sum_send,
    edge_sum_recv,
    near_send,
    near_recv,
    last_send,
    last_recv,
    tile_send,
    tile_recv,
    bar_send,
    bar_recv,
    line_send,
    line_recv,
    edge_line_send,
    edge_line_recv,
    met_sem,
):
    splits = (split_even, split_odd)
    times, levels, rows, pitch, lats, lons, owners, share, scaling = dims
    steps = rows // SUB
    lat, lon = lax.axis_index("lat"), lax.axis_index("lon")
    fields = times * levels
    last = rows - 1
    mine = pl.ds(pl.multiple_of(lon * SUB, SUB), SUB)
    places = round(math.log(lons, FAN))
    flat_flow = flow.reshape(fields * rows, LANES)
    flat_sums = sums.reshape(levels * pitch, LANES)
    flat_mean = mean_warmth.reshape(levels * rows, LANES)
    flat_warmth = warmth.reshape(fields * pitch, LANES)

    def flow_copy(n):
        part = pl.ds(pl.multiple_of(n * SUB, SUB), SUB)
        return pltpu.make_async_copy(flow_hbm.at[:, part], flow.at[:, part], flow_sem.at[n])

    def warmth_copy(n):
        part = pl.ds(pl.multiple_of(n * SUB, SUB), SUB)
        return pltpu.make_async_copy(warmth_hbm.at[:, part], warmth.at[:, part], warmth_sem.at[n])

    smalls = [
        pltpu.make_async_copy(flag_hbm, flag, small_sem.at[0]),
        pltpu.make_async_copy(floor_hbm, floor, small_sem.at[1]),
        pltpu.make_async_copy(label_hbm, label, small_sem.at[2]),
    ]
    warmth_copy(0).start()
    for copy in smalls:
        copy.start()

    barrier = pltpu.get_barrier_semaphore()
    turned_digits = [
        [lax.rem(lon // FAN**d + i, FAN) * FAN**d for i in range(FAN)] for d in range(places)
    ]
    is_owner = lon < owners

    def far_first():
        ways = itertools.product(range(FAN), repeat=places)
        hops = lambda way: sum(min(i, FAN - i) for i in way[1:]) + (way[0] > 0)
        return [way for way in sorted(ways, key=hops, reverse=True) if any(way)]

    def at(way):
        return sum(turned_digits[d][way[d]] for d in range(places))

    def signal(semaphore, way):
        pl.semaphore_signal(semaphore, inc=1, device_id=(lat, at(way)), device_id_type=MESH)

    def line_ways(d):
        return [way for way in far_first() if way[d] and sum(i > 0 for i in way) == 1]

    @pl.when(is_owner)
    def _():
        for way in far_first():
            signal(barrier, way)

    @pl.when(jnp.logical_not(is_owner))
    def _():
        for d in range(places):
            for way in line_ways(d):
                signal(barrier, way)

    @pl.when(lat < lats - 1)
    def _():
        pl.semaphore_signal(barrier, inc=1, device_id=(lat + 1, lon), device_id_type=MESH)

    for n in range(1, steps):
        warmth_copy(n).start()
    for a in range(fields // SUB):
        flat_warmth[pl.ds(a * SUB * pitch + rows, SUB, stride=pitch), :] = jnp.zeros(
            (SUB, LANES), jnp.float32
        )
    for k in range(levels):
        flat_sums[k * pitch + rows : k * pitch + rows + SUB, :] = jnp.zeros(
            (SUB, LANES), jnp.float32
        )
    depth[rows : rows + SUB, :] = jnp.zeros((SUB, LANES), jnp.int32)
    own_chip = pl.ds(pl.multiple_of(lon // CORES * SUB, SUB), SUB)
    tiles_in[own_chip, :] = jnp.zeros((SUB, LANES), jnp.float32)
    for copy in smalls:
        copy.wait()
    warmth_copy(0).wait()
    for n in range(steps):
        flow_copy(n).start()
    depth[0:rows, :] = flag[...] * floor[...]
    lane = lax.broadcasted_iota(jnp.int32, (SUB, LANES), 1)
    sub = lax.broadcasted_iota(jnp.int32, (SUB, LANES), 0)
    slots = times + 2
    turned = (lane + GROUP * sub) % LANES
    marks = [(turned >= BASINS * m) & (turned < BASINS * (m + 1)) for m in range(slots)]

    def two_parts(x):
        high = x.astype(jnp.bfloat16)
        return high, (x - high.astype(jnp.float32)).astype(jnp.bfloat16)

    def straight(x):
        return pltpu.roll(x, 0, axis=1, stride=GROUP, stride_axis=0)

    def hot_rows(n):
        iota = lax.broadcasted_iota(jnp.int32, (GROUP, LANES), 0)
        tags = label[n * SUB : (n + 1) * SUB, :]
        hot = jnp.concatenate(
            [
                jnp.where(
                    jnp.broadcast_to(tags[r : r + 1, :], (GROUP, LANES)) == iota, 1.0, 0.0
                )
                for r in (0, *range(SUB - 1, 0, -1))
            ],
            axis=0,
        ).astype(jnp.bfloat16)
        return jnp.concatenate([hot, hot], axis=1)

    def summed_over(data, hot):
        return lax.dot_general(
            data, hot, (((1,), (1,)), ((), ())), preferred_element_type=jnp.float32
        )

    def piece(out, c, m):
        x = out[c * SUB : (c + 1) * SUB, :]
        return pltpu.roll(x, BASINS * m, axis=1) if m else x

    def sum_times(n):
        here = pl.ds(n * SUB, SUB)
        for k in range(levels):
            sums[k, here, :] = functools.reduce(
                jnp.add, [warmth[t * levels + k, here, :] for t in range(times)]
            )

    for n in range(1, steps):
        warmth_copy(n).wait()
    for n in range(steps):
        sum_times(n)
    for n in range(steps):
        here = pl.ds(n * SUB, SUB)
        lim = jnp.minimum(depth[here, :], depth[pl.ds(n * SUB + 1, SUB), :])
        limit[here, :] = lim
        chunks = []
        for k in range(levels):
            wet = jnp.where(lim > k, 1.0, 0.0)
            mean_w = (sums[k, here, :] + flat_sums[pl.ds(k * pitch + n * SUB + 1, SUB), :]) * (
                0.5 / times
            )
            mean_warmth[k, here, :] = mean_w
            chunks += [wet, mean_w * wet]
        data = jnp.concatenate(two_parts(jnp.concatenate(chunks, axis=0)), axis=1)
        out = summed_over(data, hot_rows(n))
        line = jnp.zeros((SUB, LANES), jnp.float32)
        for k in range(levels):
            line = jnp.where(marks[k], piece(out, 2 * k, k), line)
            line = jnp.where(marks[levels + k], piece(out, 2 * k + 1, levels + k), line)
        line = straight(line)
        lines[n * SUB // share : (n + 1) * SUB // share] = line.reshape(
            SUB // share, share, LANES
        )

    edge_sum[...] = jnp.concatenate(
        [flat_sums[pl.ds(0, levels, stride=pitch), :], depth[0:levels, :].astype(jnp.float32)],
        axis=0,
    )
    edge_sum_copy = pltpu.make_async_remote_copy(
        src_ref=edge_sum,
        dst_ref=edge_sum_in,
        send_sem=edge_sum_send,
        recv_sem=edge_sum_recv,
        device_id=(lat - 1, lon),
        device_id_type=MESH,
    )
    edge_copy = pltpu.make_async_remote_copy(
        src_ref=edge,
        dst_ref=edge_in,
        send_sem=edge_send,
        recv_sem=edge_recv,
        device_id=(lat - 1, lon),
        device_id_type=MESH,
    )
    owner_slots = owners // FAN ** (places - 1)
    met = jnp.where(
        is_owner,
        owners - 1 + FAN - owner_slots,
        owners + (places - 1) * (FAN - 1) + FAN - 1 - owner_slots,
    )
    pl.semaphore_wait(barrier, jnp.where(lat > 0, met + 1, met))

    @pl.when(lat > 0)
    def _():
        edge_sum_copy.start()

    for way in line_ways(1):
        signal(met_sem.at[0], way)

    def to_device(src, dst, send_sem, recv_sem, device):
        return pltpu.make_async_remote_copy(
            src_ref=src,
            dst_ref=dst,
            send_sem=send_sem,
            recv_sem=recv_sem,
            device_id=(lat, device),
            device_id_type=MESH,
        )

    inner = FAN ** (places - 1)
    for way in [*far_first(), (0,) * places]:
        if way[-1] == 0:
            for first_digit in range(owner_slots):
                owner = at(way) - turned_digits[-1][0] + first_digit * inner

                def start(owner=owner):
                    to_device(
                        lines.at[owner], lines_in.at[lon], line_send, line_recv, owner
                    ).start()

                if any(way):
                    start()
                else:
                    pl.when(owner != lon)(start)

    @pl.when(is_owner)
    def _():
        lines_in[pl.ds(lon, 1)] = lines[pl.ds(lon, 1)]

    for a in range(fields // SUB):
        edge[a * SUB : (a + 1) * SUB, :] = flat_warmth[pl.ds(a * SUB * pitch, SUB, stride=pitch), :]

    @pl.when(lat > 0)
    def _():
        edge_copy.start()

    width = 2 * times + 4

    def prepare(n):
        row = n * SUB
        here = pl.ds(row, SUB)
        split = splits[n % 2]
        lim = limit[here, :]
        for k in range(levels):
            wet = jnp.where(lim > k, 1.0, 0.0)
            v = [flow[t * levels + k, here, :] for t in range(times)]
            w = [
                0.5
                * (
                    warmth[t * levels + k, here, :]
                    + flat_warmth[pl.ds((t * levels + k) * pitch + row + 1, SUB), :]
                )
                for t in range(times)
            ]
            mean_v = functools.reduce(jnp.add, v) * (1.0 / times)
            mean_w = mean_warmth[k, here, :]
            cross = functools.reduce(
                jnp.add, [(v[t] - mean_v) * (w[t] - mean_w) for t in range(times)]
            ) * (1.0 / times)
            chunks = [x * wet for x in v] + [x * wet for x in w]
            chunks += [wet, mean_v * mean_w * wet, cross * wet, jnp.zeros_like(wet)]
            for c in range(0, width, 2):
                high, low = two_parts(jnp.concatenate(chunks[c : c + 2], axis=0))
                at_row = (k * width + c) * SUB
                split[at_row : at_row + 2 * SUB, 0:LANES] = high
                split[at_row : at_row + 2 * SUB, LANES : 2 * LANES] = low

    def contract(n):
        out = summed_over(splits[n % 2][...], hot_rows(n))
        for k in range(levels):
            count = piece(out, k * width + 2 * times, times)
            for half in range(2):
                acc = jnp.where(marks[times], count, 0.0)
                for t in range(times):
                    acc = jnp.where(marks[t], piece(out, k * width + half * times + t, t), acc)
                both = piece(out, k * width + 2 * times + 1 + half, times + 1)
                acc = jnp.where(marks[times + 1], both, acc)
                tiles[pl.ds(n * SUB * SUB + half * levels + k, SUB, stride=SUB), :] = straight(acc)

    def last_hot(size):
        iota = lax.broadcasted_iota(jnp.int32, (size, LANES), 0)
        tags = jnp.broadcast_to(label[last : last + 1, :], (size, LANES))
        hot = jnp.where(tags == iota, 1.0, 0.0).astype(jnp.bfloat16)
        return jnp.concatenate([hot, hot], axis=1)

    def edge_line_of_sums():
        lim = jnp.minimum(
            depth[last : last + 1, :], edge_sum_in[levels : levels + 1, :].astype(jnp.int32)
        )
        limit[last : last + 1, :] = lim
        wet = jnp.where(jnp.broadcast_to(lim, (SUB, LANES)) > sub % levels, 1.0, 0.0)
        here = flat_sums[pl.ds(last, levels, stride=pitch), :]
        mean = (here + edge_sum_in[0:levels, :]) * (0.5 / times)
        flat_mean[pl.ds(last, levels, stride=rows), :] = mean
        chunk = wet * jnp.concatenate([jnp.ones_like(mean), mean], axis=0)
        data = jnp.concatenate(two_parts(jnp.concatenate([chunk] * 2, axis=0)), axis=1)
        return in_one_row(summed_over(data, last_hot(LANES))[0:SUB, :])

    def edge_tile():
        lim = limit[last : last + 1, :]
        wet = jnp.where(jnp.broadcast_to(lim, (SUB, LANES)) > sub % levels, 1.0, 0.0)
        x = []
        for t in range(times):
            v = flat_flow[pl.ds(t * levels * rows + last, levels, stride=rows), :]
            w = flat_warmth[pl.ds(t * levels * pitch + last, levels, stride=pitch), :]
            w = 0.5 * (w + edge_in[t * levels : (t + 1) * levels, :])
            x.append(jnp.concatenate([v, w], axis=0))
        mean = functools.reduce(jnp.add, x) * (1.0 / times)
        devs = [y - mean for y in x]
        cross = functools.reduce(jnp.add, [y * other_half(y) for y in devs]) * (1.0 / times)
        both = jnp.where(sub < levels, mean * other_half(mean), cross)
        chunks = jnp.concatenate([y * wet for y in x] + [wet, both * wet], axis=0)
        data = jnp.concatenate(two_parts(chunks), axis=1)
        out = summed_over(data, last_hot(LANES))
        return functools.reduce(jnp.add, [piece(out, m, m) for m in range(slots)])

    def other_half(x):
        return pltpu.roll(x, levels, axis=0)

    def over_sublanes(x):
        for shift in (4, 2, 1):
            x = x + pltpu.roll(x, shift, axis=0)
        return x

    def in_one_row(x):
        return over_sublanes(pltpu.roll(x, 0, axis=1, stride=BASINS, stride_axis=0))[0:1, :]

    def wait_for(ref, count, send_sem, recv_sem):
        part = pl.ds(0, count)
        return pltpu.make_async_remote_copy(
            src_ref=ref.at[part],
            dst_ref=ref.at[part],
            send_sem=send_sem,
            recv_sem=recv_sem,
            device_id=(lat, lon),
            device_id_type=MESH,
        )

    cuts = (0, steps // 2, steps)
    for low_cut, high_cut in itertools.pairwise(cuts):
        for n in range(low_cut, high_cut):
            flow_copy(n).wait()
        for n in range(low_cut, high_cut):
            prepare(n)
            if n:
                contract(n - 1)
        if high_cut < steps:
            pl.semaphore_wait(met_sem.at[0], FAN - 1)
            for way in line_ways(places - 1):
                signal(met_sem.at[1], way)
    contract(steps - 1)
    core = lax.rem(lon, CORES)
    partner = lon + 1 - CORES * core

    def tile(ref, row):
        return ref.at[pl.ds(pl.multiple_of(row * SUB, SUB), SUB)]

    pairs = rows // CORES
    for i in range(pairs):
        to_device(
            tile(tiles, CORES * i + 1 - core), tile(tiles_near, i), near_send, near_recv, partner
        ).start()

    every_line = wait_for(lines_in, lons - 1, line_send, line_recv)
    sent_lines = wait_for(lines, owners, line_send, line_recv)
    fewer_sent_lines = wait_for(lines, owners - 1, line_send, line_recv)
    sent_bars = wait_for(lines_in, lons - 1, bar_send, bar_recv)
    every_bar = wait_for(bar_in, owners, bar_send, bar_recv)
    fewer_bars = wait_for(bar_in, owners - 1, bar_send, bar_recv)
    every_edge_line = wait_for(edge_lines, lons - 1, edge_line_send, edge_line_recv)
    every_near = wait_for(tiles_near, pairs * SUB, near_send, near_recv)
    every_tile = wait_for(tiles_in, (pairs - 1) * SUB, tile_send, tile_recv)
    fewer_tiles = wait_for(tiles_in, (pairs - 2) * SUB, tile_send, tile_recv)
    every_last = wait_for(tiles_last, (lons - 1) * SUB, last_send, last_recv)

    def tree_sum(parts):
        while len(parts) > 1:
            parts = [sum(parts[i : i + 2][1:], parts[i]) for i in range(0, len(parts), 2)]
        return parts[0]

    def ratio(total):
        return total / jnp.maximum(pltpu.roll(total, levels * BASINS, axis=1), 1.0)

    pl.semaphore_wait(met_sem.at[1], FAN - 1)

    every_near.wait_recv()
    for i in range(pairs):
        own = pl.ds(pl.multiple_of((CORES * i + core) * SUB, SUB), SUB)
        tiles[own, :] = tiles[own, :] + tiles_near[i * SUB : (i + 1) * SUB, :]
    for way in far_first():
        if way[0] % CORES == 0:
            peer = at(way)

            @pl.when(peer != last)
            def _():
                to_device(
                    tile(tiles, peer), tile(tiles_in, lon // CORES), tile_send, tile_recv, peer
                ).start()

    @pl.when(lat < lats - 1)
    def _():
        edge_sum_copy.wait_recv()

    @pl.when(lat == lats - 1)
    def _():
        edge_sum_in[...] = jnp.zeros_like(edge_sum_in)

    line = edge_line_of_sums()
    edge_line[...] = line
    edge_lines[pl.ds(lon, 1)] = line.reshape(1, 1, LANES)
    for peer in map(at, far_first()):
        to_device(edge_line, edge_lines.at[lon], edge_line_send, edge_line_recv, peer).start()

    @pl.when(is_owner)
    def _():
        every_line.wait_recv()
        bar[...] = ratio(tree_sum([lines_in[p] for p in range(lons)]))
        bar_in[pl.ds(lon, 1)] = bar[...][None]
        for peer in map(at, far_first()):
            to_device(bar, bar_in.at[lon], bar_send, bar_recv, peer).start()

    @pl.when(lat < lats - 1)
    def _():
        edge_copy.wait_recv()

    @pl.when(lat == lats - 1)
    def _():
        edge_in[...] = jnp.zeros_like(edge_in)

    last_tile[...] = edge_tile()
    tiles_last[mine, :] = last_tile[...]

    @pl.when(lon != last)
    def _():
        to_device(last_tile, tile(tiles_last, lon), last_send, last_recv, last).start()

    def tiles_of(ref, count):
        return [ref[SUB * p : SUB * (p + 1), :] for p in range(count)]

    @pl.when(lon != last)
    def _():
        every_tile.wait_recv()
        own_total[...] = tree_sum([tiles[mine, :], *tiles_of(tiles_in, pairs)])

    @pl.when(lon == last)
    def _():
        every_last.wait_recv()
        own_total[...] = tree_sum(tiles_of(tiles_last, lons))

    total = own_total[...]

    def moved(x, lanes):
        return pltpu.roll(x, (-lanes) % LANES, axis=1)

    count = moved(total, BASINS * times)
    first = lane < BASINS
    divisor = jnp.maximum(count, 1.0)
    time_sums = total
    for t in range(1, times):
        time_sums = time_sums + moved(total, BASINS * t)
    bars = jnp.where(first, time_sums / divisor * (1.0 / times), 0.0)

    bars_w = other_half(bars)
    flow_part = scaling * count * bars * bars_w
    swing = jnp.zeros_like(total)
    for t in range(times):
        dev = (moved(total, 10 * t) if t else total) / divisor - bars
        swing = swing + dev * other_half(dev)
    swing = scaling * count * (swing * (1.0 / times))
    both = moved(total, 10 * (times + 1))
    steady = scaling * both - flow_part
    transient = scaling * other_half(both) - swing
    for q, value in enumerate((flow_part, steady, swing, transient)):
        for k in range(levels):
            transport_ref[q, k] = value[k : k + 1, 0:BASINS]

    every_edge_line.wait_recv()
    total = edge_lines[0:SUB].reshape(SUB, LANES)
    for n in range(1, steps):
        total = total + edge_lines[n * SUB : (n + 1) * SUB].reshape(SUB, LANES)
    last_bars = ratio(over_sublanes(total))
    @pl.when(is_owner)
    def _():
        fewer_bars.wait_recv()

    @pl.when(jnp.logical_not(is_owner))
    def _():
        every_bar.wait_recv()

    for n in range(steps):
        here = slice(n * SUB, (n + 1) * SUB)
        table = bar_in[n * SUB // share : (n + 1) * SUB // share].reshape(SUB, LANES)
        if n == steps - 1:
            table = jnp.where(sub == SUB - 1, last_bars, table)
        lim = limit[here, :]
        tags = label[here, :]
        for k in range(levels):
            cell = jnp.take_along_axis(
                table, tags + (levels + k) * BASINS, axis=1, mode="promise_in_bounds"
            )
            eddy_ref[k, here, :] = jnp.where(lim > k, mean_warmth[k, here, :] - cell, 0.0)

    for copies in (every_near, every_edge_line):
        copies.wait_send()

    @pl.when(is_owner)
    def _():
        fewer_sent_lines.wait_send()
        sent_bars.wait_send()

    @pl.when(jnp.logical_not(is_owner))
    def _():
        sent_lines.wait_send()

    skips_last = (core == CORES - 1) & (lon != last)

    @pl.when(skips_last)
    def _():
        fewer_tiles.wait_send()

    @pl.when(jnp.logical_not(skips_last))
    def _():
        every_tile.wait_send()

    @pl.when(lon != last)
    def _():
        wait_for(last_tile, SUB, last_send, last_recv).wait_send()

    @pl.when(lat > 0)
    def _():
        edge_copy.wait_send()
        edge_sum_copy.wait_send()


def write_out(eddy, transport, eddy_out, transport_out, sem):
    copies = [
        pltpu.make_async_copy(eddy, eddy_out, sem.at[0]),
        pltpu.make_async_copy(transport, transport_out, sem.at[1]),
    ]
    for copy in copies:
        copy.start()
    for copy in copies:
        copy.wait()


def shards(lats, lons, flow, warmth, flag, floor, label):
    times, levels, rows, cols = flow.shape
    fields = times * levels
    pitch = rows + SUB
    scaling = 1.0 / math.sqrt(cols * lons)
    owners = lons // OWNER_PART
    share = rows // owners
    dims = (times, levels, rows, pitch, lats, lons, owners, share, scaling)
    local = pl.BlockSpec(memory_space=pltpu.VMEM)
    dma = pltpu.SemaphoreType.DMA
    f32 = jnp.float32
    eddy, transport = pl.pallas_call(
        functools.partial(kernel, dims),
        out_shape=(
            pltpu.VMEM((levels, rows, cols), f32),
            pltpu.VMEM((4, levels, 1, BASINS), f32),
        ),
        in_specs=[pl.BlockSpec(memory_space=pltpu.HBM)] * 5,
        out_specs=(local, local),
        scratch_shapes=[
            pltpu.VMEM((fields, rows, cols), f32),
            pltpu.VMEM((fields, pitch, cols), f32),
            pltpu.VMEM((rows, cols), jnp.int32),
            pltpu.VMEM((rows, cols), jnp.int32),
            pltpu.VMEM((rows, cols), jnp.int32),
            pltpu.VMEM((pitch, cols), jnp.int32),
            pltpu.VMEM((rows, cols), jnp.int32),
            pltpu.VMEM((levels, rows, cols), f32),
            pltpu.VMEM((levels, pitch, cols), f32),
            pltpu.VMEM((levels * (2 * times + 4) * SUB, 2 * cols), jnp.bfloat16),
            pltpu.VMEM((levels * (2 * times + 4) * SUB, 2 * cols), jnp.bfloat16),
            pltpu.VMEM((fields, cols), f32),
            pltpu.VMEM((fields, cols), f32),
            pltpu.VMEM((2 * levels, cols), f32),
            pltpu.VMEM((2 * levels, cols), f32),
            pltpu.VMEM((rows * SUB, cols), f32),
            pltpu.VMEM((rows // CORES * SUB, cols), f32),
            pltpu.VMEM((share, cols), f32),
            pltpu.VMEM((owners, share, cols), f32),
            pltpu.VMEM((1, cols), f32),
            pltpu.VMEM((rows, 1, cols), f32),
            pltpu.VMEM((owners, share, cols), f32),
            pltpu.VMEM((lons, share, cols), f32),
            pltpu.VMEM((rows // CORES * SUB, cols), f32),
            pltpu.VMEM((rows * SUB, cols), f32),
            pltpu.VMEM((SUB, cols), f32),
            pltpu.VMEM((SUB, cols), f32),
            dma((rows // SUB,)),
            dma((rows // SUB,)),
            dma((3,)),
        ]
        + [dma] * 16
        + [
            pltpu.SemaphoreType.REGULAR((2,)),
        ],
        compiler_params=pltpu.CompilerParams(
            collective_id=0, has_side_effects=True, vmem_limit_bytes=66879488
        ),
    )(
        flow.reshape(fields, rows, cols),
        warmth.reshape(fields, rows, cols),
        flag,
        floor,
        label,
    )
    eddy, transport = pl.pallas_call(
        write_out,
        out_shape=tuple(jax.ShapeDtypeStruct(a.shape, a.dtype) for a in (eddy, transport)),
        in_specs=[local] * 2,
        out_specs=[pl.BlockSpec(memory_space=pltpu.HBM)] * 2,
        scratch_shapes=[dma((2,))],
        compiler_params=pltpu.CompilerParams(vmem_limit_bytes=2**20),
    )(eddy, transport)
    return eddy, jnp.transpose(transport, (0, 3, 1, 2))


def solution(mesh):
    return jax.shard_map(
        functools.partial(shards, mesh.shape["lat"], mesh.shape["lon"]),
        mesh=mesh,
        in_specs=(
            P(None, None, "lat", "lon"),
            P(None, None, "lat", "lon"),
            P("lat", "lon"),
            P("lat", "lon"),
            P("lat", "lon"),
        ),
        out_specs=(P(None, "lat", "lon"), P(None, None, None, ("lat", "lon"))),
        check_vma=False,
    )
```

time: 20.7 us -> 18.6 us (0.90)
  Pallas kernels: 19.9 us -> 17.8 us
    pallas_call x1, Pallas kernels: 19.2 us -> 17.1 us  [shards(): pl.pallas_call(functools.partial(kernel, dims), out_shape=(pltpu.VMEM((le...]
where the time goes in v4:
time: 18.6 us; the launch traced here: 18.4 us
  Pallas kernels  17.8 us (96%)
  between operations  0.64 us (3%)
    pallas_call x1, Pallas kernels, shards(): pl.pallas_call(functools.partial(kernel, dims), out_shape=(pltpu.VMEM((le...  17.1 us
    pallas_call x1, Pallas kernels, shards(): pl.pallas_call(write_out, out_shape=tuple((jax.ShapeDtypeStruct(a.shape,...  0.68 us

profile of v4, /device:TPU:1, one launch (start us, length us, event | category | flops | bytes accessed | tf_op | source)
XLA Modules:
  0.0 18.4 jit_solution(2767418778994167269)
XLA Ops:
  0.6 17.1 %shard_map.68 = (f32[4,64,128]{2,1,0:T(8,128)S(1)}, f32[4,4,1,10]{3,2,1,0:T(1,128)S(1)}) custom-call(f32[40,64,128]{2,1,0:T(8,128)} %bitcast.3, f32[40,64,128]{2,1,0:T(8,128)} %bitcast.4, s32[64,128]{1,0:T(8,128)} %flag_hbm.1, s32[64,128]{1,0:T(8,128)} %floor_hbm.1, s32[64,128]{1,0:T(8,128)} %label_hbm.1), custom_call_target="tpu_custom_call" | custom-call | tf_op jit(solution)/shard_map/pallas_call | solution.py:625
  17.8 0.7 %shard_map.69 = (f32[4,64,128]{2,1,0:T(8,128)}, f32[4,4,1,10]{3,2,1,0:T(1,128)}) custom-call(f32[4,64,128]{2,1,0:T(8,128)S(1)} %get-tuple-element.6.eddy, f32[4,4,1,10]{3,2,1,0:T(1,128)S(1)} %get-tuple-element.7.transport), custom_call_target="tpu_custom_call" | custom-call | tf_op jit(solution)/shard_map/pallas_call | solution.py:679

commit v5 on v4

--- a/solution.py
+++ b/solution.py
@@ -10,7 +10,7 @@
 from jax.sharding import PartitionSpec as P
 
 BASINS = 10
-OWNER_PART = 4
+OWNER_PART = 8
 CORES = 2
 FAN = 4
 GROUP = 16
@@ -60,20 +60,15 @@
     small_sem,
     edge_send,
     edge_recv,
-    edge_sum_send,
     edge_sum_recv,
-    near_send,
     near_recv,
-    last_send,
-    last_recv,
-    tile_send,
     tile_recv,
-    bar_send,
     bar_recv,
-    line_send,
     line_recv,
     edge_line_send,
     edge_line_recv,
+    sum_send,
+    mean_send,
     met_sem,
 ):
     splits = (split_even, split_odd)
@@ -91,17 +86,22 @@
 
     def flow_copy(n):
         part = pl.ds(pl.multiple_of(n * SUB, SUB), SUB)
-        return pltpu.make_async_copy(flow_hbm.at[:, part], flow.at[:, part], flow_sem.at[n])
+        return pltpu.make_async_copy(flow_hbm.at[:, part], flow.at[:, part], flow_sem.at[2 * n // steps])
 
     def warmth_copy(n):
         part = pl.ds(pl.multiple_of(n * SUB, SUB), SUB)
-        return pltpu.make_async_copy(warmth_hbm.at[:, part], warmth.at[:, part], warmth_sem.at[n])
+        return pltpu.make_async_copy(warmth_hbm.at[:, part], warmth.at[:, part], warmth_sem.at[min(n, 1) + 2 * n // steps])
 
     smalls = [
-        pltpu.make_async_copy(flag_hbm, flag, small_sem.at[0]),
-        pltpu.make_async_copy(floor_hbm, floor, small_sem.at[1]),
-        pltpu.make_async_copy(label_hbm, label, small_sem.at[2]),
+        pltpu.make_async_copy(flag_hbm, flag, small_sem),
+        pltpu.make_async_copy(floor_hbm, floor, small_sem),
+        pltpu.make_async_copy(label_hbm, label, small_sem),
     ]
+
+    def wait_rows(source, target, first, end, sem):
+        part = pl.ds(first * SUB, (end - first) * SUB)
+        pltpu.make_async_copy(source.at[:, part], target.at[:, part], sem).wait()
+
     warmth_copy(0).start()
     for copy in smalls:
         copy.start()
@@ -110,7 +110,12 @@
     turned_digits = [
         [lax.rem(lon // FAN**d + i, FAN) * FAN**d for i in range(FAN)] for d in range(places)
     ]
-    is_owner = lon < owners
+    reach = owners * CORES
+
+    def owns(device):
+        return (device < reach) & (lax.rem(device, CORES) == CORES - 1)
+
+    is_owner = owns(lon)
 
     def far_first():
         ways = itertools.product(range(FAN), repeat=places)
@@ -154,8 +159,9 @@
     depth[rows : rows + SUB, :] = jnp.zeros((SUB, LANES), jnp.int32)
     own_chip = pl.ds(pl.multiple_of(lon // CORES * SUB, SUB), SUB)
     tiles_in[own_chip, :] = jnp.zeros((SUB, LANES), jnp.float32)
-    for copy in smalls:
-        copy.wait()
+    pltpu.make_async_copy(
+        flow_hbm.at[0 : len(smalls)], flow.at[0 : len(smalls)], small_sem
+    ).wait()
     warmth_copy(0).wait()
     for n in range(steps):
         flow_copy(n).start()
@@ -203,9 +209,11 @@
                 jnp.add, [warmth[t * levels + k, here, :] for t in range(times)]
             )
 
-    for n in range(1, steps):
-        warmth_copy(n).wait()
-    for n in range(steps):
+    wait_rows(warmth_hbm, warmth, 1, steps // 2, warmth_sem.at[1])
+    for n in range(steps // 2):
+        sum_times(n)
+    wait_rows(warmth_hbm, warmth, steps // 2, steps, warmth_sem.at[2])
+    for n in range(steps // 2, steps):
         sum_times(n)
     for n in range(steps):
         here = pl.ds(n * SUB, SUB)
@@ -219,8 +227,9 @@
             )
             mean_warmth[k, here, :] = mean_w
             chunks += [wet, mean_w * wet]
-        data = jnp.concatenate(two_parts(jnp.concatenate(chunks, axis=0)), axis=1)
-        out = summed_over(data, hot_rows(n))
+        data = jnp.concatenate(two_parts(jnp.concatenate(chunks, axis=0)), axis=0)
+        out = summed_over(data, hot_rows(n)[:, 0:LANES])
+        out = out[0 : 2 * levels * SUB, :] + out[2 * levels * SUB :, :]
         line = jnp.zeros((SUB, LANES), jnp.float32)
         for k in range(levels):
             line = jnp.where(marks[k], piece(out, 2 * k, k), line)
@@ -237,7 +246,7 @@
     edge_sum_copy = pltpu.make_async_remote_copy(
         src_ref=edge_sum,
         dst_ref=edge_sum_in,
-        send_sem=edge_sum_send,
+        send_sem=edge_send,
         recv_sem=edge_sum_recv,
         device_id=(lat - 1, lon),
         device_id_type=MESH,
@@ -250,12 +259,10 @@
         device_id=(lat - 1, lon),
         device_id_type=MESH,
     )
-    owner_slots = owners // FAN ** (places - 1)
-    met = jnp.where(
-        is_owner,
-        owners - 1 + FAN - owner_slots,
-        owners + (places - 1) * (FAN - 1) + FAN - 1 - owner_slots,
-    )
+    plain = [
+        jnp.where(owns(at(way)), 0, 1) for d in range(places) for way in line_ways(d)
+    ]
+    met = sum(plain) + owners - jnp.where(is_owner, 1, 0)
     pl.semaphore_wait(barrier, jnp.where(lat > 0, met + 1, met))
 
     @pl.when(lat > 0)
@@ -276,24 +283,24 @@
         )
 
     inner = FAN ** (places - 1)
-    for way in [*far_first(), (0,) * places]:
-        if way[-1] == 0:
-            for first_digit in range(owner_slots):
-                owner = at(way) - turned_digits[-1][0] + first_digit * inner
-
-                def start(owner=owner):
-                    to_device(
-                        lines.at[owner], lines_in.at[lon], line_send, line_recv, owner
-                    ).start()
-
-                if any(way):
-                    start()
-                else:
-                    pl.when(owner != lon)(start)
+    for shift in sorted(range(FAN), key=lambda i: -min(i, FAN - i)):
+        for rest in itertools.product(range(reach // inner), range(FAN // CORES)):
+            owner = rest[0] * inner + turned_digits[1][shift] + rest[1] * CORES + CORES - 1
+
+            def start(owner=owner):
+                mine_there = lines_in.at[lon]
+                to_device(
+                    lines.at[owner // CORES], mine_there, mean_send, line_recv, owner
+                ).start()
+
+            if shift:
+                start()
+            else:
+                pl.when(owner != lon)(start)
 
     @pl.when(is_owner)
     def _():
-        lines_in[pl.ds(lon, 1)] = lines[pl.ds(lon, 1)]
+        lines_in[pl.ds(lon, 1)] = lines[pl.ds(lon // CORES, 1)]
 
     for a in range(fields // SUB):
         edge[a * SUB : (a + 1) * SUB, :] = flat_warmth[pl.ds(a * SUB * pitch, SUB, stride=pitch), :]
@@ -362,7 +369,15 @@
         flat_mean[pl.ds(last, levels, stride=rows), :] = mean
         chunk = wet * jnp.concatenate([jnp.ones_like(mean), mean], axis=0)
         data = jnp.concatenate(two_parts(jnp.concatenate([chunk] * 2, axis=0)), axis=1)
-        return in_one_row(summed_over(data, last_hot(LANES))[0:SUB, :])
+        iota = lax.broadcasted_iota(jnp.int32, (LANES, LANES), 0)
+        tags = jnp.broadcast_to(label[last : last + 1, :], (LANES, LANES))
+        inside = (iota >= levels * BASINS) & (iota < 2 * levels * BASINS)
+        hot = jnp.where(inside & (tags == iota % BASINS), 1.0, 0.0).astype(jnp.bfloat16)
+        out = summed_over(data, jnp.concatenate([hot, hot], axis=1))[0:SUB, :]
+        out = jnp.where(lane // BASINS - levels == sub % levels, out, 0.0)
+        for shift in (1, 2):
+            out = out + pltpu.roll(out, shift, axis=0)
+        return jnp.concatenate([out[levels - 1 : levels, :], out[2 * levels - 1 :, :]], axis=0)
 
     def edge_tile():
         lim = limit[last : last + 1, :]
@@ -385,14 +400,6 @@
     def other_half(x):
         return pltpu.roll(x, levels, axis=0)
 
-    def over_sublanes(x):
-        for shift in (4, 2, 1):
-            x = x + pltpu.roll(x, shift, axis=0)
-        return x
-
-    def in_one_row(x):
-        return over_sublanes(pltpu.roll(x, 0, axis=1, stride=BASINS, stride_axis=0))[0:1, :]
-
     def wait_for(ref, count, send_sem, recv_sem):
         part = pl.ds(0, count)
         return pltpu.make_async_remote_copy(
@@ -406,8 +413,7 @@
 
     cuts = (0, steps // 2, steps)
     for low_cut, high_cut in itertools.pairwise(cuts):
-        for n in range(low_cut, high_cut):
-            flow_copy(n).wait()
+        wait_rows(flow_hbm, flow, low_cut, high_cut, flow_sem.at[2 * low_cut // steps])
         for n in range(low_cut, high_cut):
             prepare(n)
             if n:
@@ -426,20 +432,16 @@
     pairs = rows // CORES
     for i in range(pairs):
         to_device(
-            tile(tiles, CORES * i + 1 - core), tile(tiles_near, i), near_send, near_recv, partner
+            tile(tiles, CORES * i + 1 - core), tile(tiles_near, i), sum_send, near_recv, partner
         ).start()
 
-    every_line = wait_for(lines_in, lons - 1, line_send, line_recv)
-    sent_lines = wait_for(lines, owners, line_send, line_recv)
-    fewer_sent_lines = wait_for(lines, owners - 1, line_send, line_recv)
-    sent_bars = wait_for(lines_in, lons - 1, bar_send, bar_recv)
-    every_bar = wait_for(bar_in, owners, bar_send, bar_recv)
-    fewer_bars = wait_for(bar_in, owners - 1, bar_send, bar_recv)
+    every_line = wait_for(lines_in, lons - 1, mean_send, line_recv)
+    every_bar = wait_for(bar_in, owners, mean_send, bar_recv)
+    fewer_bars = wait_for(bar_in, owners - 1, mean_send, bar_recv)
     every_edge_line = wait_for(edge_lines, lons - 1, edge_line_send, edge_line_recv)
-    every_near = wait_for(tiles_near, pairs * SUB, near_send, near_recv)
-    every_tile = wait_for(tiles_in, (pairs - 1) * SUB, tile_send, tile_recv)
-    fewer_tiles = wait_for(tiles_in, (pairs - 2) * SUB, tile_send, tile_recv)
-    every_last = wait_for(tiles_last, (lons - 1) * SUB, last_send, last_recv)
+    every_near = wait_for(tiles_near, pairs * SUB, sum_send, near_recv)
+    every_tile = wait_for(tiles_in, (pairs - 1) * SUB, sum_send, tile_recv)
+    every_last = wait_for(tiles_last, (lons - 1) * SUB, sum_send, tile_recv)
 
     def tree_sum(parts):
         while len(parts) > 1:
@@ -462,7 +464,7 @@
             @pl.when(peer != last)
             def _():
                 to_device(
-                    tile(tiles, peer), tile(tiles_in, lon // CORES), tile_send, tile_recv, peer
+                    tile(tiles, peer), tile(tiles_in, lon // CORES), sum_send, tile_recv, peer
                 ).start()
 
     @pl.when(lat < lats - 1)
@@ -475,7 +477,7 @@
 
     line = edge_line_of_sums()
     edge_line[...] = line
-    edge_lines[pl.ds(lon, 1)] = line.reshape(1, 1, LANES)
+    edge_lines[pl.ds(lon, 1)] = line[None]
     for peer in map(at, far_first()):
         to_device(edge_line, edge_lines.at[lon], edge_line_send, edge_line_recv, peer).start()
 
@@ -483,9 +485,9 @@
     def _():
         every_line.wait_recv()
         bar[...] = ratio(tree_sum([lines_in[p] for p in range(lons)]))
-        bar_in[pl.ds(lon, 1)] = bar[...][None]
+        bar_in[pl.ds(lon // CORES, 1)] = bar[...][None]
         for peer in map(at, far_first()):
-            to_device(bar, bar_in.at[lon], bar_send, bar_recv, peer).start()
+            to_device(bar, bar_in.at[lon // CORES], mean_send, bar_recv, peer).start()
 
     @pl.when(lat < lats - 1)
     def _():
@@ -500,7 +502,7 @@
 
     @pl.when(lon != last)
     def _():
-        to_device(last_tile, tile(tiles_last, lon), last_send, last_recv, last).start()
+        to_device(last_tile, tile(tiles_last, lon), sum_send, tile_recv, last).start()
 
     def tiles_of(ref, count):
         return [ref[SUB * p : SUB * (p + 1), :] for p in range(count)]
@@ -543,10 +545,8 @@
             transport_ref[q, k] = value[k : k + 1, 0:BASINS]
 
     every_edge_line.wait_recv()
-    total = edge_lines[0:SUB].reshape(SUB, LANES)
-    for n in range(1, steps):
-        total = total + edge_lines[n * SUB : (n + 1) * SUB].reshape(SUB, LANES)
-    last_bars = ratio(over_sublanes(total))
+    total = tree_sum([edge_lines[p] for p in range(lons)])
+    last_bars = total[1:2, :] / jnp.maximum(total[0:1, :], 1.0)
     @pl.when(is_owner)
     def _():
         fewer_bars.wait_recv()
@@ -559,7 +559,7 @@
         here = slice(n * SUB, (n + 1) * SUB)
         table = bar_in[n * SUB // share : (n + 1) * SUB // share].reshape(SUB, LANES)
         if n == steps - 1:
-            table = jnp.where(sub == SUB - 1, last_bars, table)
+            table = jnp.where(sub == SUB - 1, jnp.broadcast_to(last_bars, table.shape), table)
         lim = limit[here, :]
         tags = label[here, :]
         for k in range(levels):
@@ -568,36 +568,30 @@
             )
             eddy_ref[k, here, :] = jnp.where(lim > k, mean_warmth[k, here, :] - cell, 0.0)
 
-    for copies in (every_near, every_edge_line):
-        copies.wait_send()
+    every_edge_line.wait_send()
+
+    def wait_sent(count, semaphore):
+        wait_for(flat_flow, count, semaphore, edge_recv).wait_send()
+
+    @pl.when(core == CORES - 1)
+    def _():
+        wait_sent((2 * pairs - 1) * SUB, sum_send)
+
+    @pl.when(core < CORES - 1)
+    def _():
+        wait_sent(2 * pairs * SUB, sum_send)
 
     @pl.when(is_owner)
     def _():
-        fewer_sent_lines.wait_send()
-        sent_bars.wait_send()
+        wait_sent((owners - 1 + lons - 1) * share, mean_send)
 
     @pl.when(jnp.logical_not(is_owner))
     def _():
-        sent_lines.wait_send()
-
-    skips_last = (core == CORES - 1) & (lon != last)
-
-    @pl.when(skips_last)
-    def _():
-        fewer_tiles.wait_send()
-
-    @pl.when(jnp.logical_not(skips_last))
-    def _():
-        every_tile.wait_send()
-
-    @pl.when(lon != last)
-    def _():
-        wait_for(last_tile, SUB, last_send, last_recv).wait_send()
+        wait_sent(owners * share, mean_send)
 
     @pl.when(lat > 0)
     def _():
-        edge_copy.wait_send()
-        edge_sum_copy.wait_send()
+        wait_sent(fields + 2 * levels, edge_send)
 
 
 def write_out(eddy, transport, eddy_out, transport_out, sem):
@@ -650,19 +644,19 @@
             pltpu.VMEM((rows // CORES * SUB, cols), f32),
             pltpu.VMEM((share, cols), f32),
             pltpu.VMEM((owners, share, cols), f32),
-            pltpu.VMEM((1, cols), f32),
-            pltpu.VMEM((rows, 1, cols), f32),
+            pltpu.VMEM((2, cols), f32),
+            pltpu.VMEM((lons, 2, cols), f32),
             pltpu.VMEM((owners, share, cols), f32),
             pltpu.VMEM((lons, share, cols), f32),
             pltpu.VMEM((rows // CORES * SUB, cols), f32),
             pltpu.VMEM((rows * SUB, cols), f32),
             pltpu.VMEM((SUB, cols), f32),
             pltpu.VMEM((SUB, cols), f32),
-            dma((rows // SUB,)),
-            dma((rows // SUB,)),
+            dma((2,)),
             dma((3,)),
+            dma,
         ]
-        + [dma] * 16
+        + [dma] * 11
         + [
             pltpu.SemaphoreType.REGULAR((2,)),
         ],

time: 18.6 us -> 18.5 us (level)
  no operation moved by 1% of the time
where the time goes in v5:
time: 18.5 us; the launch traced here: 18.4 us
  Pallas kernels  17.8 us (96%)
  between operations  0.64 us (3%)
    pallas_call x1, Pallas kernels, shards(): pl.pallas_call(functools.partial(kernel, dims), out_shape=(pltpu.VMEM((le...  17.1 us
    pallas_call x1, Pallas kernels, shards(): pl.pallas_call(write_out, out_shape=tuple((jax.ShapeDtypeStruct(a.shape,...  0.68 us

profile of v5, /device:TPU:1, one launch (start us, length us, event | category | flops | bytes accessed | tf_op | source)
XLA Modules:
  0.0 18.4 jit_solution(14716124830992314796)
XLA Ops:
  0.6 17.1 %shard_map.68 = (f32[4,64,128]{2,1,0:T(8,128)S(1)}, f32[4,4,1,10]{3,2,1,0:T(1,128)S(1)}) custom-call(f32[40,64,128]{2,1,0:T(8,128)} %bitcast.3, f32[40,64,128]{2,1,0:T(8,128)} %bitcast.4, s32[64,128]{1,0:T(8,128)} %flag_hbm.1, s32[64,128]{1,0:T(8,128)} %floor_hbm.1, s32[64,128]{1,0:T(8,128)} %label_hbm.1), custom_call_target="tpu_custom_call" | custom-call | tf_op jit(solution)/shard_map/pallas_call | solution.py:619
  17.7 0.7 %shard_map.69 = (f32[4,64,128]{2,1,0:T(8,128)}, f32[4,4,1,10]{3,2,1,0:T(1,128)}) custom-call(f32[4,64,128]{2,1,0:T(8,128)S(1)} %get-tuple-element.6.eddy, f32[4,4,1,10]{3,2,1,0:T(1,128)S(1)} %get-tuple-element.7.transport), custom_call_target="tpu_custom_call" | custom-call | tf_op jit(solution)/shard_map/pallas_call | solution.py:673

commit v6 on v5

--- a/solution.py
+++ b/solution.py
@@ -138,8 +138,8 @@
 
     @pl.when(jnp.logical_not(is_owner))
     def _():
-        for d in range(places):
-            for way in line_ways(d):
+        for way in far_first():
+            if sum(i > 0 for i in way) == 1:
                 signal(barrier, way)
 
     @pl.when(lat < lats - 1)
@@ -176,6 +176,15 @@
         high = x.astype(jnp.bfloat16)
         return high, (x - high.astype(jnp.float32)).astype(jnp.bfloat16)
 
+    def in_three(x):
+        high = x.astype(jnp.bfloat16).astype(jnp.float32)
+        rest = x - high
+        middle = rest.astype(jnp.bfloat16).astype(jnp.float32)
+        return [high, middle, rest - middle]
+
+    def folded(out, size):
+        return out[0:size, :] + out[size : 2 * size, :] + out[2 * size : 3 * size, :]
+
     def straight(x):
         return pltpu.roll(x, 0, axis=1, stride=GROUP, stride_axis=0)
 
@@ -227,9 +236,9 @@
             )
             mean_warmth[k, here, :] = mean_w
             chunks += [wet, mean_w * wet]
-        data = jnp.concatenate(two_parts(jnp.concatenate(chunks, axis=0)), axis=0)
-        out = summed_over(data, hot_rows(n)[:, 0:LANES])
-        out = out[0 : 2 * levels * SUB, :] + out[2 * levels * SUB :, :]
+        data = jnp.concatenate(in_three(jnp.concatenate(chunks, axis=0)), axis=0)
+        out = summed_over(data.astype(jnp.bfloat16), hot_rows(n)[:, 0:LANES])
+        out = folded(out, 2 * levels * SUB)
         line = jnp.zeros((SUB, LANES), jnp.float32)
         for k in range(levels):
             line = jnp.where(marks[k], piece(out, 2 * k, k), line)
@@ -368,12 +377,12 @@
         mean = (here + edge_sum_in[0:levels, :]) * (0.5 / times)
         flat_mean[pl.ds(last, levels, stride=rows), :] = mean
         chunk = wet * jnp.concatenate([jnp.ones_like(mean), mean], axis=0)
-        data = jnp.concatenate(two_parts(jnp.concatenate([chunk] * 2, axis=0)), axis=1)
+        data = jnp.concatenate([*in_three(chunk), jnp.zeros_like(chunk)], axis=0)
         iota = lax.broadcasted_iota(jnp.int32, (LANES, LANES), 0)
         tags = jnp.broadcast_to(label[last : last + 1, :], (LANES, LANES))
         inside = (iota >= levels * BASINS) & (iota < 2 * levels * BASINS)
         hot = jnp.where(inside & (tags == iota % BASINS), 1.0, 0.0).astype(jnp.bfloat16)
-        out = summed_over(data, jnp.concatenate([hot, hot], axis=1))[0:SUB, :]
+        out = folded(summed_over(data.astype(jnp.bfloat16), hot), SUB)
         out = jnp.where(lane // BASINS - levels == sub % levels, out, 0.0)
         for shift in (1, 2):
             out = out + pltpu.roll(out, shift, axis=0)

time: 18.5 us -> 18.5 us (level)
  no operation moved by 1% of the time
where the time goes in v6:
time: 18.5 us; the launch traced here: 18.4 us
  Pallas kernels  17.8 us (96%)
  between operations  0.64 us (3%)
    pallas_call x1, Pallas kernels, shards(): pl.pallas_call(functools.partial(kernel, dims), out_shape=(pltpu.VMEM((le...  17.1 us
    pallas_call x1, Pallas kernels, shards(): pl.pallas_call(write_out, out_shape=tuple((jax.ShapeDtypeStruct(a.shape,...  0.68 us

profile of v6, /device:TPU:1, one launch (start us, length us, event | category | flops | bytes accessed | tf_op | source)
XLA Modules:
  0.0 18.4 jit_solution(11821779314733562525)
XLA Ops:
  0.6 17.1 %shard_map.68 = (f32[4,64,128]{2,1,0:T(8,128)S(1)}, f32[4,4,1,10]{3,2,1,0:T(1,128)S(1)}) custom-call(f32[40,64,128]{2,1,0:T(8,128)} %bitcast.3, f32[40,64,128]{2,1,0:T(8,128)} %bitcast.4, s32[64,128]{1,0:T(8,128)} %flag_hbm.1, s32[64,128]{1,0:T(8,128)} %floor_hbm.1, s32[64,128]{1,0:T(8,128)} %label_hbm.1), custom_call_target="tpu_custom_call" | custom-call | tf_op jit(solution)/shard_map/pallas_call | solution.py:628
  17.7 0.7 %shard_map.69 = (f32[4,64,128]{2,1,0:T(8,128)}, f32[4,4,1,10]{3,2,1,0:T(1,128)}) custom-call(f32[4,64,128]{2,1,0:T(8,128)S(1)} %get-tuple-element.6.eddy, f32[4,4,1,10]{3,2,1,0:T(1,128)S(1)} %get-tuple-element.7.transport), custom_call_target="tpu_custom_call" | custom-call | tf_op jit(solution)/shard_map/pallas_call | solution.py:682

commit v7 on v6

--- a/solution.py
+++ b/solution.py
@@ -604,14 +604,12 @@
 
 
 def write_out(eddy, transport, eddy_out, transport_out, sem):
-    copies = [
-        pltpu.make_async_copy(eddy, eddy_out, sem.at[0]),
-        pltpu.make_async_copy(transport, transport_out, sem.at[1]),
-    ]
-    for copy in copies:
-        copy.start()
-    for copy in copies:
-        copy.wait()
+    for k in range(eddy.shape[0]):
+        pltpu.make_async_copy(eddy.at[k], eddy_out.at[k], sem.at[0]).start()
+    small = pltpu.make_async_copy(transport, transport_out, sem.at[1])
+    small.start()
+    pltpu.make_async_copy(eddy, eddy_out, sem.at[0]).wait()
+    small.wait()
 
 
 def shards(lats, lons, flow, warmth, flag, floor, label):

time: 18.5 us -> 18.5 us (level)
  no operation moved by 1% of the time
where the time goes in v7:
time: 18.5 us; the launch traced here: 18.4 us
  Pallas kernels  17.8 us (96%)
  between operations  0.64 us (3%)
    pallas_call x1, Pallas kernels, shards(): pl.pallas_call(functools.partial(kernel, dims), out_shape=(pltpu.VMEM((le...  17.1 us
    pallas_call x1, Pallas kernels, shards(): pl.pallas_call(write_out, out_shape=tuple((jax.ShapeDtypeStruct(a.shape,...  0.67 us

profile of v7, /device:TPU:1, one launch (start us, length us, event | category | flops | bytes accessed | tf_op | source)
XLA Modules:
  0.0 18.4 jit_solution(8951614043316158302)
XLA Ops:
  0.6 17.1 %shard_map.68 = (f32[4,64,128]{2,1,0:T(8,128)S(1)}, f32[4,4,1,10]{3,2,1,0:T(1,128)S(1)}) custom-call(f32[40,64,128]{2,1,0:T(8,128)} %bitcast.3, f32[40,64,128]{2,1,0:T(8,128)} %bitcast.4, s32[64,128]{1,0:T(8,128)} %flag_hbm.1, s32[64,128]{1,0:T(8,128)} %floor_hbm.1, s32[64,128]{1,0:T(8,128)} %label_hbm.1), custom_call_target="tpu_custom_call" | custom-call | tf_op jit(solution)/shard_map/pallas_call | solution.py:626
  17.7 0.7 %shard_map.69 = (f32[4,64,128]{2,1,0:T(8,128)}, f32[4,4,1,10]{3,2,1,0:T(1,128)}) custom-call(f32[4,64,128]{2,1,0:T(8,128)S(1)} %get-tuple-element.6.eddy, f32[4,4,1,10]{3,2,1,0:T(1,128)S(1)} %get-tuple-element.7.transport), custom_call_target="tpu_custom_call" | custom-call | tf_op jit(solution)/shard_map/pallas_call | solution.py:680
